TPU v7x, 32 devices: a 4x4x1 block of a 4x4x8 slice. The times are simulated.
32 devices in a mesh: dp: 1 (over z), ep: 32 (over y, x, core).
Axes of the slice: x: 4, y: 4, z: 1, core: 2. Of those that a mesh axis runs over, the one named last changes fastest.
The devices are a block of a 4x4x8 slice.
Arguments:
- x_in: bfloat16 [32768, 1024], P(('dp', 'ep'))
- expert_ids: int32 [32768, 8], P(('dp', 'ep'))
- norm_weight: bfloat16 [1024], replicated
- router_w: bfloat16 [1024, 32], replicated
- router_b: bfloat16 [32], replicated
- w_gate_up: bfloat16 [32, 1024, 1024], P('ep')
- b_gate_up: bfloat16 [32, 1024], P('ep')
- w_down: bfloat16 [32, 512, 1024], P('ep')
- b_down: bfloat16 [32, 1024], P('ep')
Outputs:
- output: bfloat16 [32768, 1024], P(('dp', 'ep'))
All inputs are finite; a program needn't handle non-finite values.
Results may differ from a plain program's by a relative error of at most 0.00637158.
Values are sent between devices in bfloat16 or wider.
A program may use at most 768 MiB of HBM per device.

v0:
```python
import jax
import jax.numpy as jnp
from jax import lax
from jax.sharding import PartitionSpec as P

CAPACITY_FACTOR = 4
EPSILON = 1e-5
LIMIT = 7.0
ALPHA = 1.702


def rms_norm(x_in, norm_weight):
    x_float = x_in.astype(jnp.float32)
    inv_rms = lax.rsqrt(jnp.mean(x_float * x_float, axis=-1, keepdims=True) + EPSILON)
    return (x_float * inv_rms * norm_weight.astype(jnp.float32)).astype(jnp.bfloat16)


def route_gates(hidden, expert_ids, router_w, router_b):
    logits = jnp.dot(hidden, router_w, preferred_element_type=jnp.float32) + router_b.astype(jnp.float32)
    return jax.nn.softmax(jnp.take_along_axis(logits, expert_ids, axis=1), axis=-1)


def clamped_glu(gate_up):
    gate = jnp.minimum(gate_up[..., 0::2].astype(jnp.float32), LIMIT)
    linear = jnp.clip(gate_up[..., 1::2].astype(jnp.float32), -LIMIT, LIMIT)
    return (gate * jax.nn.sigmoid(ALPHA * gate) * (linear + 1.0)).astype(jnp.bfloat16)


def slot_tables(flat_ids, experts, capacity):
    pairs = flat_ids.shape[0]
    onehot = (flat_ids[:, None] == jnp.arange(experts, dtype=jnp.int32)[None, :]).astype(jnp.int32)
    rank = jnp.sum((jnp.cumsum(onehot, axis=0) - 1) * onehot, axis=1)
    slot_pair = jnp.zeros((experts * capacity,), jnp.int32).at[flat_ids * capacity + rank].set(jnp.arange(pairs, dtype=jnp.int32))
    return slot_pair, rank, jnp.sum(onehot, axis=0)


def mix_residual(x_in, gates, picked):
    mixed = jnp.sum(gates[:, :, None] * picked.astype(jnp.float32), axis=1)
    return (x_in.astype(jnp.float32) + mixed).astype(jnp.bfloat16)


def solution(mesh):
    n_group = mesh.shape['ep']
    rows_spec = P(('dp', 'ep'), None)

    def local_block(x_in, expert_ids, norm_weight, router_w, router_b, w_gate_up, b_gate_up, w_down, b_down):
        tok_dev, d_model = x_in.shape
        top_k = expert_ids.shape[1]
        local_exp = w_gate_up.shape[0]
        experts = local_exp * n_group
        capacity = CAPACITY_FACTOR * top_k * tok_dev // experts
        hidden = rms_norm(x_in, norm_weight)
        gates = route_gates(hidden, expert_ids, router_w, router_b)
        flat_ids = expert_ids.reshape(-1)
        slot_pair, rank, _ = slot_tables(flat_ids, experts, capacity)
        rows = jnp.take(hidden, slot_pair // top_k, axis=0).reshape(n_group, local_exp, capacity, d_model)
        received = lax.all_to_all(rows, 'ep', 0, 0, tiled=True)
        gate_up = (jnp.einsum('sgcd,gdf->gscf', received, w_gate_up, preferred_element_type=jnp.float32) + b_gate_up[:, None, None, :].astype(jnp.float32)).astype(jnp.bfloat16)
        expert_out = (jnp.einsum('gscf,gfd->gscd', clamped_glu(gate_up), w_down, preferred_element_type=jnp.float32) + b_down[:, None, None, :].astype(jnp.float32)).astype(jnp.bfloat16)
        returned = lax.all_to_all(expert_out, 'ep', 1, 1, tiled=True)
        back_slot = ((flat_ids % local_exp) * n_group + flat_ids // local_exp) * capacity + rank
        picked = jnp.take(returned.reshape(-1, d_model), back_slot, axis=0).reshape(tok_dev, top_k, d_model)
        return mix_residual(x_in, gates, picked)

    return jax.shard_map(local_block, mesh=mesh, in_specs=(rows_spec, rows_spec, P(), P(), P(), P('ep', None, None), P('ep', None), P('ep', None, None), P('ep', None)), out_specs=rows_spec, check_vma=False)
```

profile of v0, /device:TPU:97, one launch (start us, length us, event | category | flops | bytes accessed | tf_op | source)
XLA Modules:
  0.0 4717.0 jit_solution(12438835141256222290)
XLA Ops:
  0.0 0.9 broadcast_multiply_fusion
  0.9 0.9 copy.33
  1.9 0.3 eq.28
  2.1 0.3 reshape.181
  2.4 0.2 copy.37
  2.6 0.3 mul.77
  2.9 1.1 fusion.18
  4.0 17.1 reduce-window.6
  21.1 0.9 slice_reduce_fusion
  22.0 0.2 reduce-window.9
  22.2 0.3 add_add_fusion
  22.6 0.8 fusion.16
  23.4 0.1 compare_select_fusion.1
  23.4 0.0 copy-start.8
  23.4 0.5 copy-done.5
  24.0 30.5 scatter_custom_fusion
  54.5 0.1 compare_and_fusion
  54.6 0.1 broadcast_clamp_fusion
  54.7 0.7 convert_element_type.68
  55.4 2.1 fusion.10
  57.5 0.6 broadcast_in_dim.44
  58.1 3.5 fusion.12
  61.6 161.0 %gather_fusion = bf16[32768,1024]{1,0:T(8,128)(2,1)} fusion(bf16[1024,1024]{1,0:T(8,128)(2,1)} %fusion.12, s32[32768]{0:T(1024)S(1)} %broadcast_clamp_fusion), kind=kCustom, calls=%fused_computation | custom fusion | bytes 134348800 | tf_op jit(solution)/shard_map/jit(_take)/gather | solution.py:56
  222.6 44.4 broadcast_select_fusion
  267.0 9.2 all-to-all-start
  276.3 0.6 convert_element_type.86
  276.9 827.3 %all-to-all-done = bf16[32,1,1024,1024]{3,2,1,0:T(8,128)(2,1)} async-done(((bf16[32,1,1024,1024]{3,2,1,0:T(8,128)(2,1)}), bf16[32,1,1024,1024]{3,2,1,0:T(8,128)(2,1)}, u32[]{:S(2)}, u32[]{:S(2)}) %all-to-all-start) | async-done | bytes 67108896 | tf_op jit(solution)/shard_map/all_to_all | solution.py:57
  1104.2 78.1 %fusion = bf16[1,32,1024,1024]{3,2,1,0:T(8,128)(2,1)} fusion(f32[1024]{0:T(1024)S(1)} %bitcast.65, bf16[32,1,1024,1024]{3,2,1,0:T(8,128)(2,1)} %all-to-all-done, bf16[1,1024,1024]{2,1,0:T(8,128)(2,1)S(1)} %copy-done), kind=kOutput, calls=%fused_computation.6 | convolution fusion | flops 68786585600 | bytes 136318976 | tf_op jit(solution)/shard_map/sgcd,gdf->gscf/dot_general | solution.py:58
  1182.2 1201.8 %slice.15 = bf16[1,32,1024,512]{3,2,1,0:T(8,128)(2,1)} slice(bf16[1,32,1024,1024]{3,2,1,0:T(8,128)(2,1)} %fusion), slice={[0:1:1], [0:32:1], [0:1024:1], [1:1024:2]} | slice | bytes 67108864 | tf_op jit(solution)/shard_map/slice | solution.py:25
  2384.1 1202.1 %slice.14 = bf16[1,32,1024,512]{3,2,1,0:T(8,128)(2,1)} slice(bf16[1,32,1024,1024]{3,2,1,0:T(8,128)(2,1)} %fusion), slice={[0:1:1], [0:32:1], [0:1024:1], [0:1024:2]} | slice | bytes 67108864 | tf_op jit(solution)/shard_map/slice | solution.py:24
  3586.2 58.2 %fusion.1 = bf16[1,32,1024,1024]{3,2,0,1:T(8,128)(2,1)} fusion(f32[1024]{0:T(1024)S(1)} %bitcast.64, bf16[1,32,1024,512]{3,2,1,0:T(8,128)(2,1)} %slice.15, bf16[1,32,1024,512]{3,2,1,0:T(8,128)(2,1)} %slice.14, bf16[1,512,1024]{2,1,0:T(8,128)(2,1)S(1)} %copy-done.14), kind=kOutput, calls=%fused_computation.7 | convolution fusion | flops 34628173824 | bytes 135270400 | tf_op jit(solution)/shard_map/gscf,gfd->gscd/dot_general | solution.py:59
  3644.4 0.0 copy-start.10
  3644.4 74.3 %all-to-all-start.1 = ((bf16[1,32,1024,1024]{3,2,0,1:T(8,128)(2,1)}), bf16[1,32,1024,1024]{3,2,0,1:T(8,128)(2,1)}, u32[]{:S(2)}, u32[]{:S(2)}) async-start(bf16[1,32,1024,1024]{3,2,0,1:T(8,128)(2,1)} %fusion.1), calls=%async_computation.1 | async-start | bytes 134217728 | tf_op jit(solution)/shard_map/all_to_all | solution.py:60
  3718.7 0.3 reduce_sum.43
  3719.1 0.2 copy.30
  3719.3 0.3 reshape.206
  3719.5 0.2 copy.35
  3719.7 0.9 copy.36
  3720.6 2.3 convolution_add_fusion
  3722.9 0.0 copy-start.3
  3722.9 65.5 %gather_fusion.2 = f32[8192]{0:T(1024)S(1)} fusion(f32[1024,32]{0,1:T(8,128)S(1)} %convolution_add_fusion, s32[8192]{0:T(1024)S(1)} %reshape.206), kind=kCustom, calls=%fused_computation.2 | custom fusion | bytes 131072 | tf_op jit(solution)/shard_map/jit(take_along_axis)/gather | solution.py:20
  3788.5 0.3 reshape.209
  3788.8 0.2 copy.31
  3789.0 0.2 copy.32
  3789.3 756.5 %all-to-all-done.1 = bf16[1,32,1024,1024]{3,2,0,1:T(8,128)(2,1)} async-done(((bf16[1,32,1024,1024]{3,2,0,1:T(8,128)(2,1)}), bf16[1,32,1024,1024]{3,2,0,1:T(8,128)(2,1)}, u32[]{:S(2)}, u32[]{:S(2)}) %all-to-all-start.1) | async-done | bytes 67108896 | tf_op jit(solution)/shard_map/all_to_all | solution.py:60
  4545.8 150.6 %gather_fusion.1 = bf16[8192,1024]{1,0:T(8,128)(2,1)} fusion(bf16[32768,1024]{1,0:T(8,128)(2,1)} %bitcast.17, s32[8192]{0:T(1024)S(1)} %broadcast_clamp_fusion.1), kind=kCustom, calls=%fused_computation.1 | custom fusion | bytes 33587200 | tf_op jit(solution)/shard_map/jit(_take)/gather | solution.py:62
  4696.3 16.9 multiply_reduce_fusion
  4713.3 3.8 fusion.13
  (38 shorter events, 0.2 us)
Async XLA Ops:
  0.0 1104.2 %copy-start = (bf16[1,1024,1024]{2,1,0:T(8,128)(2,1)S(1)}, bf16[1,1024,1024]{2,1,0:T(8,128)(2,1)}, u32[]{:S(2)}) copy-start(bf16[1,1024,1024]{2,1,0:T(8,128)(2,1)} %param.14) | copy-start | bytes 6291460
  23.4 0.6 copy-start.5
  23.4 31.0 copy-start.8
  61.6 161.0 %copy-start.7 = (pred[32,1024]{1,0:T(8,128)(4,1)S(1)}, pred[32,1024]{1,0:T(8,128)(4,1)}, u32[]{:S(2)}) copy-start(pred[32,1024]{1,0:T(8,128)(4,1)} %broadcast_in_dim.44) | copy-start | bytes 98308
  267.0 9.2 copy-start.11
  267.0 9.3 copy-start.12
  267.0 837.1 %all-to-all-start = ((bf16[32,1,1024,1024]{3,2,1,0:T(8,128)(2,1)}), bf16[32,1,1024,1024]{3,2,1,0:T(8,128)(2,1)}, u32[]{:S(2)}, u32[]{:S(2)}) async-start(bf16[32,1,1024,1024]{3,2,1,0:T(8,128)(2,1)} %broadcast_select_fusion), calls=%async_computation | async-start | bytes 134217728 | tf_op jit(solution)/shard_map/all_to_all | solution.py:57
  2384.1 1202.1 %copy-start.13 = (f32[1,1024]{1,0:T(1,128)S(1)}, f32[1,1024]{1,0:T(1,128)}, u32[]{:S(2)}) copy-start(f32[1,1024]{1,0:T(1,128)} %convert_element_type.86) | copy-start | bytes 12292
  2384.1 1202.1 %copy-start.14 = (bf16[1,512,1024]{2,1,0:T(8,128)(2,1)S(1)}, bf16[1,512,1024]{2,1,0:T(8,128)(2,1)}, u32[]{:S(2)}) copy-start(bf16[1,512,1024]{2,1,0:T(8,128)(2,1)} %param.16) | copy-start | bytes 3145732
  3644.4 74.3 %copy-start.6 = (s32[8192]{0:T(1024)S(1)}, s32[8192]{0:T(1024)}, u32[]{:S(2)}) copy-start(s32[8192]{0:T(1024)} %copy-done.5) | copy-start | bytes 98308
  3644.4 74.6 %copy-start.15 = (bf16[32]{0:T(256)(128)(2,1)S(1)}, bf16[32]{0:T(256)(128)(2,1)}, u32[]{:S(2)}) copy-start(bf16[32]{0:T(256)(128)(2,1)} %param.13) | copy-start | bytes 196
  3644.4 74.6 %copy-start.2 = (s32[1024,8]{0,1:T(8,128)S(1)}, s32[1024,8]{0,1:T(8,128)}, u32[]{:S(2)}) copy-start(s32[1024,8]{0,1:T(8,128)} %param.10) | copy-start | bytes 98308
  3644.4 76.2 %copy-start.10 = (bf16[1024,32]{0,1:T(8,128)(2,1)S(1)}, bf16[1024,32]{0,1:T(8,128)(2,1)}, u32[]{:S(2)}) copy-start(bf16[1024,32]{0,1:T(8,128)(2,1)} %param.12) | copy-start | bytes 196612
  3644.4 901.3 %all-to-all-start.1 = ((bf16[1,32,1024,1024]{3,2,0,1:T(8,128)(2,1)}), bf16[1,32,1024,1024]{3,2,0,1:T(8,128)(2,1)}, u32[]{:S(2)}, u32[]{:S(2)}) async-start(bf16[1,32,1024,1024]{3,2,0,1:T(8,128)(2,1)} %fusion.1), calls=%async_computation.1 | async-start | bytes 134217728 | tf_op jit(solution)/shard_map/all_to_all | solution.py:60
  3722.9 66.0 %copy-start.3 = (s32[1024,8]{0,1:T(8,128)S(1)}, s32[1024,8]{0,1:T(8,128)}, u32[]{:S(2)}) copy-start(s32[1024,8]{0,1:T(8,128)} %param.10) | copy-start | bytes 98308
  3722.9 66.3 %copy-start.9 = (s32[8192,1]{0,1:T(1,128)S(1)}, s32[8192,1]{0,1:T(1,128)}, u32[]{:S(2)}) copy-start(s32[8192,1]{0,1:T(1,128)} %copy-done.8) | copy-start | bytes 98308
  4545.8 150.6 %copy-start.4 = (pred[1024,8]{1,0:T(8,128)(4,1)S(1)}, pred[1024,8]{1,0:T(8,128)(4,1)}, u32[]{:S(2)}) copy-start(pred[1024,8]{1,0:T(8,128)(4,1)} %copy.36) | copy-start | bytes 24580
  4545.8 171.3 %copy-start.1 = (bf16[1,1024,1024]{2,1,0:T(8,128)(2,1)S(1)}, bf16[1,1024,1024]{2,1,0:T(8,128)(2,1)}, u32[]{:S(2)}) copy-start(bf16[1,1024,1024]{2,1,0:T(8,128)(2,1)} %param.14) | copy-start | bytes 6291460
where the time goes:
time: 4790 us; the launch traced here: 4720 us
  local copies, waits for them, and re-layouts  2820 us (59%)
  waiting for transfers between devices  1580 us (33%)
  matrix products  139 us (3%)
  other arithmetic  92.8 us (2%)
  starting transfers between devices  83.5 us (2%)
    slice x1, local copies, waits for them, and re-layouts, clamped_glu(): gate = jnp.minimum(gate_up[..., 0::2].astype(jnp.float32), LIMIT)  1200 us
    slice x1, local copies, waits for them, and re-layouts, clamped_glu(): linear = jnp.clip(gate_up[..., 1::2].astype(jnp.float32), -LIMIT, LIMIT)  1200 us
    all_to_all x1, waiting for transfers between devices, local_block(): received = lax.all_to_all(rows, 'ep', 0, 0, tiled=True)  827 us
    all_to_all x1, waiting for transfers between devices, local_block(): returned = lax.all_to_all(expert_out, 'ep', 1, 1, tiled=True)  756 us
    gather x1, local copies, waits for them, and re-layouts, local_block(): jnp.take(hidden, slot_pair // top_k, axis=0)  161 us
    gather x1, local copies, waits for them, and re-layouts, local_block(): jnp.take(returned.reshape(-1, d_model), back_slot, axis=0)  151 us
  transfers between devices with their start and end apart: 2, of which 2 were waited for; matrix products, arithmetic and copies ran while one was open for 2% of the time, Pallas kernels for 0%

commit v1 on v0

v1 whole, which is shorter than its diff:
```python
import functools
import math

import jax
import jax.numpy as jnp
from jax import lax
from jax.experimental import pallas as pl
from jax.experimental.pallas import tpu as pltpu
from jax.sharding import PartitionSpec as P

EPSILON = 1e-5
LIMIT = 7.0
ALPHA = 1.702
F32, BF16 = jnp.float32, jnp.bfloat16
MESH = pl.DeviceIdType.MESH
COLS = 256
RING = 4
ORDER = [(0, 0), (0, 3), (0, 1), (1, 0), (0, 2), (1, 3), (1, 1), (1, 2)]
SLOTS = 2 * len(ORDER)


def kernel(x_hbm, ids_v, norm_v, rw_v, rb_v, wgu_hbm, bgu_v, wd_hbm, bd_v, out_hbm, wg, wd, z_v, h_v, wbuf, g_v, gsend, acc, rs_v, x_v, ostage, bias_v, rwp_v, wg_s, wg_r, wd_s, wd_r, bias_s, bias_r, hg_s, hg_r, rs_s, rs_r, ld_sem, ld2_sem, in_sem, out_sem):
    tok, d_model = x_hbm.shape
    d_ff = wd_hbm.shape[1]
    groups = 2 * d_ff // COLS
    half_g = groups // 2
    blocks = d_model // COLS
    tm = tok // 2
    top_k = ids_v.shape[1]
    me = lax.axis_index('ep')
    core = lax.rem(me, 2)
    col = lax.rem(me // 2, RING)
    row = me // (2 * RING)
    away = 1 - 2 * core

    def dev(dy, dx, flip=0):
        other = 1 - core if flip else core
        return {'ep': (lax.rem(row + dy + RING, RING) * RING + lax.rem(col + dx + RING, RING)) * 2 + other}

    peers = [(2 * s, dc, f) for s, dc in ORDER for f in (0, 1)][1:]
    for dy, dx, f in peers + [(1, 0, 0), (-1, 0, 0)]:
        pl.semaphore_signal(pltpu.get_barrier_semaphore(), 1, device_id=dev(dy, dx, f), device_id_type=MESH)

    def remote(src, dst, ssem, rsem, where):
        return pltpu.make_async_remote_copy(src_ref=src, dst_ref=dst, send_sem=ssem, recv_sem=rsem, device_id=where, device_id_type=MESH)

    routes = {2: (0, 1), 4: (0, -1), 6: (0, 'y'), 10: (6, 1), 12: (6, -1)}
    relays = {8: ((2, 1), (4, -1)), 14: ((10, 1), (12, -1))}

    def route(q, part):
        if not isinstance(q, int):
            return q - 1, 'sib'
        if q % 2:
            return q - 1, 'sib'
        return relays[q][part] if q in relays else routes[q]

    def target(way):
        if way == 'sib':
            return dev(0, 0, 1)
        return dev(2, 0) if way == 'y' else dev(0, way)

    def gate_up(q, ch):
        src, way = route(q, ch)
        part = pl.ds(half_g * ch, half_g)
        own = isinstance(src, int) and src == 0
        return remote(wbuf.at[part] if own else wg.at[src, part], wg.at[q, part], wg_s.at[q, ch], wg_r.at[q, ch], target(way))

    def down(q, j, half=None):
        src, way = route(q, half)
        here = wd_hbm.at[0, :, pl.ds(pl.multiple_of(j * COLS, COLS), COLS)] if isinstance(src, int) and src == 0 else wd.at[src, j]
        there = wd.at[q, j]
        if half is not None:
            rows = pl.ds(d_ff // 2 * half, d_ff // 2)
            here, there = wd.at[src, j, rows], wd.at[q, j, rows]
        at = 0 if half is None else half
        return remote(here, there, wd_s.at[q, j, at], wd_r.at[q, j, at], target(way))

    def hidden_send():
        return remote(h_v.at[pl.ds(tok, tok)], h_v.at[pl.ds(0, tok)], hg_s.at[0], hg_r.at[0], dev(away, 0))

    def gates_send():
        return remote(gsend, g_v.at[pl.ds(0, tok)], hg_s.at[1], hg_r.at[1], dev(away, 0))

    def bias_send(q, where):
        return remote(bias_v.at[0], bias_v.at[q], bias_s.at[q], bias_r.at[q], where)

    def sum_send(j, t):
        return remote(acc.at[lax.rem(j, 2), t], rs_v.at[j, t], rs_s.at[j, t], rs_r.at[j, t], dev(-away, 0))

    raw = h_v.at[pl.ds(tok, tok)]
    load_w = pltpu.make_async_copy(wgu_hbm.at[0], raw.at[pl.ds(0, d_model)], in_sem.at[0])
    load_x = pltpu.make_async_copy(x_hbm, x_v, in_sem.at[1])
    load_w.start()
    load_x.start()

    ri = lax.broadcasted_iota(jnp.int32, (COLS, COLS), 0)
    ci = lax.broadcasted_iota(jnp.int32, (COLS, COLS), 1)
    split = jnp.where(ri == jnp.where(ci < COLS // 2, 2 * ci, 2 * ci - (COLS - 1)), 1.0, 0.0).astype(BF16)
    load_w.wait()
    for ch in range(2):
        for g in range(half_g * ch, half_g * (ch + 1)):
            wbuf[g] = jnp.dot(raw[pl.ds(0, d_model), COLS * g:COLS * (g + 1)], split, preferred_element_type=F32).astype(BF16)
        if ch == 0:
            pl.semaphore_wait(pltpu.get_barrier_semaphore(), len(peers) + 2)
        for q in (2, 4, 6, 1):
            gate_up(q, ch).start()

    for g in range(groups):
        b = jnp.dot(jnp.broadcast_to(bgu_v[:, COLS * g:COLS * (g + 1)], (16, COLS)), split, preferred_element_type=F32)
        bias_v[0, 2 * g:2 * g + 1, :] = b[0:1, :128]
        bias_v[0, 2 * g + 1:2 * g + 2, :] = b[0:1, 128:]
    for i in range(d_model // 128):
        bias_v[0, 2 * groups + i:2 * groups + i + 1, :] = bd_v[:, 128 * i:128 * (i + 1)].astype(F32)
    bias_msgs = []
    for s, dc in ORDER:
        for f in (0, 1):
            q = 2 * ORDER.index((s, (RING - dc) % RING)) + f
            if q:
                bias_msgs.append(bias_send(q, dev(2 * s, dc, f)))
                bias_msgs[-1].start()

    lane = lax.broadcasted_iota(jnp.int32, (1, 128), 1)
    slot = lane & (SLOTS - 1)
    class_row = jnp.where(lane < SLOTS, row, row + away + RING)
    far = jnp.zeros_like(lane)
    side = jnp.zeros_like(lane)
    for m, (s, dc) in enumerate(ORDER):
        far = jnp.where(slot // 2 == m, 2 * s, far)
        side = jnp.where(slot // 2 == m, dc, side)
    expert = (((class_row + far) & (RING - 1)) * RING + ((col + side) & (RING - 1))) * 2 + jnp.where((slot & 1) == 1, 1 - core, core)
    expert = jnp.where(lane < 2 * SLOTS, expert, -1)
    n_exp = rw_v.shape[1]
    pick = jnp.where(lax.broadcasted_iota(jnp.int32, (n_exp, 128), 0) == expert, 1.0, 0.0).astype(BF16)
    rwp_v[...] = jnp.dot(rw_v[...], pick, preferred_element_type=F32).astype(BF16)
    rb_p = jnp.dot(jnp.broadcast_to(rb_v[...], (16, n_exp)), pick, preferred_element_type=F32)[0:1]
    load_x.wait()
    norm = norm_v[...].astype(F32)
    tn = tok // 4

    @pl.loop(0, 4)
    def _(i):
        rows = pl.ds(pl.multiple_of(i * tn, tn), tn)
        own = pl.ds(pl.multiple_of(tok + i * tn, tn), tn)
        xf = x_v[rows, :].astype(F32)
        inv = lax.rsqrt(jnp.mean(xf * xf, axis=-1, keepdims=True) + EPSILON)
        hidden = (xf * inv * norm).astype(BF16)
        h_v[own, :] = hidden
        logits = jnp.dot(hidden, rwp_v[...], preferred_element_type=F32) + rb_p
        ids = ids_v[rows, :]
        chosen = ids[:, 0:1] == expert
        for e in range(1, top_k):
            chosen = chosen | (ids[:, e:e + 1] == expert)
        top = jnp.max(jnp.where(chosen, logits, -jnp.inf), axis=-1, keepdims=True)
        weight = jnp.where(chosen, jnp.exp(logits - top), 0.0)
        gates = weight / jnp.sum(weight, axis=-1, keepdims=True)
        g_v[own, :] = gates
        gsend[rows, :] = pltpu.roll(gates, 128 - SLOTS, 1)

    hidden_send().start()
    gates_send().start()
    for j in range(blocks):
        down(6, j).start()
        down(1, j).start()

    def q_of(s):
        return jnp.where(s < SLOTS, lax.rem(s, SLOTS // 2), SLOTS // 2 + (s - SLOTS) // 2)

    def own_of(s):
        return jnp.where(s < SLOTS, s < SLOTS // 2, lax.rem(s, 2) == 0)

    def set_of(s):
        return jnp.where(q_of(s) == 0, 0, 1 + lax.rem(s, 3))

    def weights_load(s):
        return pltpu.make_async_copy(wg.at[q_of(s)], wbuf.at[pl.ds(groups * set_of(s), groups)], ld_sem.at[set_of(s)])

    def landed(*msgs):
        for q, ch in msgs:
            gate_up(q, ch).wait_recv()

    def go(*msgs):
        for q, ch in msgs:
            gate_up(q, ch).start()

    def down_go(j, *qs):
        for q in qs:
            down(q, j).start()

    def down_landed(j, *qs):
        for q in qs:
            down(q, j).wait_recv()

    def event_1():
        landed((2, 0), (4, 0))
        go((8, 0), (3, 0), (5, 0))
        landed((2, 1), (4, 1))
        go((8, 1), (3, 1), (5, 1))

    def event_5():
        landed((6, 0), (6, 1))
        go((10, 0), (12, 0), (10, 1), (12, 1), (7, 0), (7, 1))

    def event_7():
        hidden_send().wait_recv()
        gates_send().wait_recv()

    def event_9():
        landed((8, 0), (8, 1))
        go((9, 0), (9, 1))

    def event_17():
        landed((10, 0), (12, 0))
        go((14, 0), (11, 0), (13, 0))

    def event_19():
        landed((10, 1), (12, 1))
        go((14, 1), (11, 1), (13, 1))
        for j in range(blocks):
            down_landed(j, 6)
            down_go(j, 7)
        down_go(0, 2, 4, 10, 12)
        down_go(1, 2, 4)

    def event_27():
        landed((14, 0), (14, 1))
        go((15, 0), (15, 1))

    events = {1: event_1, 5: event_5, 7: event_7, 9: event_9, 17: event_17, 19: event_19, 27: event_27}
    for msg in bias_msgs:
        msg.wait_recv()

    @pl.loop(0, 4 * SLOTS)
    def _(i):
        s = i // 2
        t = lax.rem(i, 2)
        q = q_of(s)

        @pl.when((t == 0) & (q > 0))
        def _():
            weights_load(s).wait()

        @pl.when(t == 1)
        def _():
            for at, event in events.items():
                pl.when(s == at)(event)
            nxt = s + 1
            q1 = q_of(nxt)

            @pl.when((lax.rem(q1, 2) == 1) & own_of(nxt) & (nxt < 2 * SLOTS))
            def _():
                for ch in range(2):
                    gate_up(q1, ch).wait_recv()

            @pl.when((q1 > 0) & (nxt < 2 * SLOTS))
            def _():
                weights_load(nxt).start()

        base = jnp.where(own_of(s), tok, 0)
        rows = pl.ds(pl.multiple_of(base + t * tm, tm), tm)
        w_at = groups * set_of(s)
        for g in range(groups):
            u = jnp.dot(h_v[rows, :], wbuf[w_at + g], preferred_element_type=F32)
            a = (u[:, :128] + bias_v[q, 2 * g:2 * g + 1, :]).astype(BF16)
            l = (u[:, 128:] + bias_v[q, 2 * g + 1:2 * g + 2, :]).astype(BF16)
            a = jnp.minimum(a, LIMIT).astype(F32)
            l = jnp.clip(l, -LIMIT, LIMIT).astype(F32)
            z_v[q, rows, 128 * g:128 * (g + 1)] = (a * jax.nn.sigmoid(ALPHA * a) * (l + 1.0)).astype(BF16)

    for q in (2, 4, 6, 1):
        for ch in range(2):
            gate_up(q, ch).wait_send()

    def down_load(j, q):
        spot = wbuf.at[SLOTS // 2 * lax.rem(j, 2) + q // 2, pl.ds(d_ff * (q % 2), d_ff)]
        src = wd_hbm.at[0, :, pl.ds(pl.multiple_of(j * COLS, COLS), COLS)] if q == 0 else wd.at[q, j]
        return pltpu.make_async_copy(src, spot, ld2_sem.at[lax.rem(j, 2), q])

    def direct(j):
        down_landed(j, 2, 4, 10, 12)
        for q in (8, 14):
            for half in range(2):
                down(q, j, half).start()

        @pl.when(j + 1 < blocks)
        def _():
            down_go(j + 1, 10, 12)

        @pl.when(j + 2 < blocks)
        def _():
            down_go(j + 2, 2, 4)

        down_go(j, 3, 5, 11, 13)
        for q in (0, 2, 4, 6, 10, 12):
            down_load(j, q).start()

    def relayed(j):
        for q in (8, 14):
            for half in range(2):
                down(q, j, half).wait_recv()
        down_go(j, 9, 15)
        for q in (8, 14):
            down_load(j, q).start()
        for q in (1, 3, 5, 7, 11, 13, 9, 15):
            down(q, j).wait_recv()
            down_load(j, q).start()
        for q in range(SLOTS):
            down_load(j, q).wait()

    def out_copy(j, t):
        cols = pl.ds(pl.multiple_of(j * COLS, COLS), COLS)
        return pltpu.make_async_copy(ostage.at[t], out_hbm.at[pl.ds(t * tm, tm), cols], out_sem.at[t])

    def finish(j, wait_out):
        cols = pl.ds(pl.multiple_of(j * COLS, COLS), COLS)
        for t in range(2):
            sum_send(j, t).wait_recv()
            if wait_out is not None:
                pl.when(wait_out)(lambda t=t: out_copy(j - 1, t).wait())
            total = acc[lax.rem(j, 2), 2 + t] + rs_v[j, t]
            ostage[t] = (x_v[pl.ds(t * tm, tm), cols].astype(F32) + total).astype(BF16)
            out_copy(j, t).start()

    direct(0)

    @pl.loop(0, blocks)
    def _(j):
        relayed(j)
        par = lax.rem(j, 2)

        @pl.loop(0, 4)
        def _(t):
            @pl.when((t < 2) & (j >= 2))
            def _():
                sum_send(j - 2, t).wait_send()

            @pl.when((t == 2) & (j + 1 < blocks))
            def _():
                direct(j + 1)

            @pl.when((t == 3) & (j >= 1))
            def _():
                finish(j - 1, j >= 2)

            rows = pl.ds(pl.multiple_of(t * tm, tm), tm)
            total = None
            for e in range(SLOTS):
                w = wbuf[SLOTS // 2 * par + e // 2, d_ff * (e % 2):d_ff * (e % 2 + 1), :]
                y = jnp.dot(z_v[e, rows, :], w, preferred_element_type=F32)
                b = jnp.concatenate([bias_v[e, pl.ds(2 * groups + 2 * j, 1), :], bias_v[e, pl.ds(2 * groups + 2 * j + 1, 1), :]], axis=1)
                y = (y + b).astype(BF16).astype(F32)
                p = g_v[rows, e:e + 1]
                term = jnp.where(p > 0, y * p, 0.0)
                total = term if total is None else total + term
            acc[par, t] = total

            @pl.when(t < 2)
            def _():
                sum_send(j, t).start()

    finish(blocks - 1, blocks >= 2)
    for t in range(2):
        out_copy(blocks - 1, t).wait()
        for j in range(max(blocks - 2, 0), blocks):
            sum_send(j, t).wait_send()

    for q in range(SLOTS):
        for ch in range(2):
            if q not in (0, 1, 2, 4, 6):
                gate_up(q, ch).wait_send()
        for j in range(blocks):
            if q in relays:
                for half in range(2):
                    down(q, j, half).wait_send()
            elif q:
                down(q, j).wait_send()
    for msg in bias_msgs:
        msg.wait_send()
    hidden_send().wait_send()
    gates_send().wait_send()


def solution(mesh):
    rows_spec = P(('dp', 'ep'), None)
    assert mesh.shape['ep'] == 2 * RING * RING

    def local_block(x_in, expert_ids, norm_weight, router_w, router_b, w_gate_up, b_gate_up, w_down, b_down):
        tok, d_model = x_in.shape
        d_ff = w_down.shape[1]
        assert w_gate_up.shape[0] == 1 and tok >= d_model
        groups, blocks, tm = 2 * d_ff // COLS, d_model // COLS, tok // 2
        hbm = pl.BlockSpec(memory_space=pltpu.HBM)
        vmem = pl.BlockSpec(memory_space=pltpu.VMEM)
        dma = pltpu.SemaphoreType.DMA
        wide = max(groups * 4, SLOTS * d_ff // d_model * 2)
        out = pl.pallas_call(
            kernel,
            out_shape=(
                jax.ShapeDtypeStruct((tok, d_model), BF16),
                jax.ShapeDtypeStruct((SLOTS, groups, d_model, COLS), BF16),
                jax.ShapeDtypeStruct((SLOTS, blocks, d_ff, COLS), BF16),
            ),
            in_specs=[hbm, vmem, vmem, vmem, vmem, hbm, vmem, hbm, vmem],
            out_specs=(hbm, hbm, hbm),
            scratch_shapes=[
                pltpu.VMEM((SLOTS, 2 * tok, d_ff), BF16),
                pltpu.VMEM((2 * tok, d_model), BF16),
                pltpu.VMEM((wide, d_model, COLS), BF16),
                pltpu.VMEM((2 * tok, 128), F32),
                pltpu.VMEM((tok, 128), F32),
                pltpu.VMEM((2, 4, tm, COLS), F32),
                pltpu.VMEM((blocks, 2, tm, COLS), F32),
                pltpu.VMEM((tok, d_model), BF16),
                pltpu.VMEM((2, tm, COLS), BF16),
                pltpu.VMEM((SLOTS, 2 * groups + d_model // 128, 128), F32),
                pltpu.VMEM((d_model, 128), BF16),
                dma((SLOTS, 2)),
                dma((SLOTS, 2)),
                dma((SLOTS, blocks, 2)),
                dma((SLOTS, blocks, 2)),
                dma((SLOTS,)),
                dma((SLOTS,)),
                dma((2,)),
                dma((2,)),
                dma((blocks, 2)),
                dma((blocks, 2)),
                dma((4,)),
                dma((2, SLOTS)),
                dma((2,)),
                dma((2,)),
            ],
            compiler_params=pltpu.CompilerParams(collective_id=0, has_side_effects=True, vmem_limit_bytes=67043328),
        )(x_in, expert_ids, norm_weight[None], router_w, router_b[None], w_gate_up, b_gate_up, w_down, b_down)
        return out[0]

    return jax.shard_map(local_block, mesh=mesh, in_specs=(rows_spec, rows_spec, P(), P(), P(), P('ep', None, None), P('ep', None), P('ep', None, None), P('ep', None)), out_specs=rows_spec, check_vma=False)
```

time: 4790 us -> 266 us (0.06); the launches traced: 4720 us -> 265 us
  local copies, waits for them, and re-layouts: 2820 us -> 7.79 us
  waiting for transfers between devices: 1580 us -> 0 us
  Pallas kernels: 0 us -> 257 us
  matrix products: 139 us -> 0 us
  other arithmetic: 92.8 us -> 0 us
  starting transfers between devices: 83.5 us -> 0 us
    slice x3 -> x0, local copies, waits for them, and re-layouts: 2400 us -> none  [the longest x1 1200 us: clamped_glu(): gate = jnp.minimum(gate_up[..., 0::2].astype(jnp.float32), LIMIT)]
    all_to_all x2 -> x0, waiting for transfers between devices: 1580 us -> none  [the longest x1 827 us: local_block(): received = lax.all_to_all(rows, 'ep', 0, 0, tiled=True)]
    gather x7 -> x0, local copies, waits for them, and re-layouts: 378 us -> none  [the longest x1 161 us: local_block(): jnp.take(hidden, slot_pair // top_k, axis=0)]
    pallas_call x0 -> x1, Pallas kernels: none -> 257 us  [local_block(): pl.pallas_call(kernel, out_shape=(jax.ShapeDtypeStruct((tok, d_model), BF...]
    dot_general x3 -> x0, matrix products: 139 us -> none  [the longest x1 78.1 us: local_block(): jnp.einsum('sgcd,gdf->gscf', received, w_gate_up, preferred_element_type=...]
    all_to_all x2 -> x0, starting transfers between devices: 83.5 us -> none  [the longest x1 74.3 us: local_block(): returned = lax.all_to_all(expert_out, 'ep', 1, 1, tiled=True)]
  transfers between devices with their start and end apart: 2 -> 0, of which waited for: 2 -> 0; matrix products, arithmetic and copies ran while one was open for 2% -> 0% of each run, Pallas kernels for 0% -> 0%
where the time goes in v1:
time: 266 us; the launch traced here: 265 us
  Pallas kernels  257 us (97%)
  local copies, waits for them, and re-layouts  7.79 us (3%)
    pallas_call x1, Pallas kernels, local_block(): pl.pallas_call(kernel, out_shape=(jax.ShapeDtypeStruct((tok, d_model), BF...  257 us
    unnamed x3, local copies, waits for them, and re-layouts  6.51 us

profile of v1, /device:TPU:97, one launch (start us, length us, event | category | flops | bytes accessed | tf_op | source)
XLA Modules:
  0.0 264.7 jit_solution(16363589176757592462)
XLA Ops:
  0.0 1.3 broadcast_in_dim.6.norm_v
  1.3 1.7 copy.11.rw_v
  3.0 1.8 copy.10.ids_v
  4.7 256.9 %shard_map.91 = (bf16[1024,1024]{1,0:T(8,128)(2,1)}, bf16[16,4,1024,256]{3,2,1,0:T(8,128)(2,1)}, bf16[16,4,512,256]{3,2,1,0:T(8,128)(2,1)}) custom-call(bf16[1024,1024]{1,0:T(8,128)(2,1)} %x_hbm.1, s32[1024,8]{1,0:T(8,128)} %copy.10.ids_v, bf16[1,1024]{1,0:T(2,128)(2,1)} %broadcast_in_dim.6.norm_v, bf16[1024,32]{1,0:T(8,128)(2,1)} %copy.11.rw_v, ...), custom_call_target="tpu_custom_call" | custom-call | tf_op jit(solution)/shard_map/pallas_call | solution.py:395
  261.6 3.1 %copy.13 = bf16[1024,1024]{1,0:T(8,128)(2,1)} copy(bf16[1024,1024]{1,0:T(8,128)(2,1)} %get-tuple-element.6) | data formatting | bytes 4194304

commit v2 on v1

v2 whole, which is shorter than its diff:
```python
import jax
import jax.numpy as jnp
from jax import lax
from jax.experimental import pallas as pl
from jax.experimental.pallas import tpu as pltpu
from jax.sharding import PartitionSpec as P

EPSILON = 1e-5
LIMIT = 7.0
ALPHA = 1.702
F32, BF16 = jnp.float32, jnp.bfloat16
MESH = pl.DeviceIdType.MESH
COLS = 256
RING = 4
ORDER = [(0, 0), (0, 3), (0, 1), (1, 0), (0, 2), (1, 3), (1, 1), (1, 2)]
SLOTS = 2 * len(ORDER)


def kernel(x_hbm, ids_v, norm_v, rw_v, rb_v, wgu_hbm, bgu_v, wd_hbm, bd_v, out_hbm, wg, wd, z_v, h_v, wbuf, g_v, gfar, gsend, acc, rs_v, x_v, ostage, bias_v, rwp_v, wg_s, wg_r, wd_s, wd_r, bias_s, bias_r, hg_s, hg_r, rs_s, rs_r, ld_sem, ld2_sem, in_sem, out_sem):
    tok, d_model = x_hbm.shape
    d_ff = wd_hbm.shape[1]
    groups = 2 * d_ff // COLS
    half_g = groups // 2
    blocks = d_model // COLS
    tm = tok // 2
    top_k = ids_v.shape[0]
    me = lax.axis_index('ep')
    core = lax.rem(me, 2)
    col = lax.rem(me // 2, RING)
    row = me // (2 * RING)
    away = 1 - 2 * core
    scope = jax.named_scope

    def dev(dy, dx, flip=0):
        other = 1 - core if flip else core
        return {'ep': (lax.rem(row + dy + RING, RING) * RING + lax.rem(col + dx + RING, RING)) * 2 + other}

    peers = [(2 * s, dc, f) for s, dc in ORDER for f in (0, 1)][1:]
    for dy, dx, f in peers + [(1, 0, 0), (-1, 0, 0)]:
        pl.semaphore_signal(pltpu.get_barrier_semaphore(), 1, device_id=dev(dy, dx, f), device_id_type=MESH)

    def remote(src, dst, ssem, rsem, where):
        return pltpu.make_async_remote_copy(src_ref=src, dst_ref=dst, send_sem=ssem, recv_sem=rsem, device_id=where, device_id_type=MESH)

    gate_up_way = {(2, 0): (0, 1), (2, 1): (0, 1), (4, 0): (0, -1), (4, 1): (0, -1), (6, 0): (0, 'y'), (6, 1): (0, 'y'), (8, 0): (4, -1), (8, 1): (2, 1),
                   (10, 0): (6, 1), (10, 1): (2, 'y'), (12, 0): (6, -1), (12, 1): (4, 'y'), (14, 0): (12, -1), (14, 1): (10, 1)}
    down_way = {2: (0, 1), 4: (0, -1), 6: (0, 'y'), (8, 0): (2, 1), (8, 1): (4, -1), 10: (6, 1), 12: (6, -1), (14, 0): (10, 1), (14, 1): (12, -1)}
    relayed_slots = (8, 14)

    def target(way):
        if way == 'sib':
            return dev(0, 0, 1)
        return dev(2, 0) if way == 'y' else dev(0, way)

    def gate_up(q, ch):
        src, way = gate_up_way.get((q, ch), (None, 'sib')) if isinstance(q, int) else (None, 'sib')
        part = pl.ds(half_g * ch, half_g)
        if src == 0 or (isinstance(q, int) and q == 1):
            here = wbuf.at[part]
        else:
            here = wg.at[q - 1 if src is None else src, part]
        return remote(here, wg.at[q, part], wg_s.at[q, ch], wg_r.at[q, ch], target(way))

    def down(q, j, half=None):
        src, way = down_way.get(q if half is None else (q, half), (q - 1, 'sib'))
        rows = slice(None) if half is None else pl.ds(d_ff // 2 * half, d_ff // 2)
        here = wd_hbm.at[0, :, pl.ds(pl.multiple_of(j * COLS, COLS), COLS)] if src == 0 else wd.at[src, j, rows]
        at = 0 if half is None else half
        return remote(here, wd.at[q, j, rows], wd_s.at[q, j, at], wd_r.at[q, j, at], target(way))

    def hidden_send():
        return remote(h_v.at[pl.ds(tok, tok)], h_v.at[pl.ds(0, tok)], hg_s.at[0], hg_r.at[0], dev(away, 0))

    def gates_send():
        return remote(gsend, gfar, hg_s.at[1], hg_r.at[1], dev(away, 0))

    def bias_send(q, where):
        return remote(bias_v.at[0], bias_v.at[q], bias_s.at[q], bias_r.at[q], where)

    def sum_send(j, t):
        return remote(acc.at[lax.rem(j, 2), t], rs_v.at[j, t], rs_s.at[j, t], rs_r.at[j, t], dev(-away, 0))

    raw = h_v.at[pl.ds(tok, tok)]
    load_w = pltpu.make_async_copy(wgu_hbm.at[0], raw.at[pl.ds(0, d_model)], in_sem.at[0])
    load_x = pltpu.make_async_copy(x_hbm, x_v, in_sem.at[1])
    load_w.start()
    load_x.start()

    ri = lax.broadcasted_iota(jnp.int32, (COLS, COLS), 0)
    ci = lax.broadcasted_iota(jnp.int32, (COLS, COLS), 1)
    split = jnp.where(ri == jnp.where(ci < COLS // 2, 2 * ci, 2 * ci - (COLS - 1)), 1.0, 0.0).astype(BF16)
    for g in range(groups):
        b = jnp.dot(jnp.broadcast_to(bgu_v[:, COLS * g:COLS * (g + 1)], (16, COLS)), split, preferred_element_type=F32)
        bias_v[0, 2 * g:2 * g + 1, :] = b[0:1, :128]
        bias_v[0, 2 * g + 1:2 * g + 2, :] = b[0:1, 128:]
    for i in range(d_model // 128):
        bias_v[0, 2 * groups + i:2 * groups + i + 1, :] = bd_v[:, 128 * i:128 * (i + 1)].astype(F32)
    with scope('load_w'):
        load_w.wait()
    for g in range(groups):
        wbuf[g] = jnp.dot(raw[pl.ds(0, d_model), COLS * g:COLS * (g + 1)], split, preferred_element_type=F32).astype(BF16)
    with scope('barrier'):
        pl.semaphore_wait(pltpu.get_barrier_semaphore(), len(peers) + 2)
    bias_msgs = []
    for s, dc in ORDER:
        for f in (0, 1):
            q = 2 * ORDER.index((s, (RING - dc) % RING)) + f
            if q:
                bias_msgs.append(bias_send(q, dev(2 * s, dc, f)))
                bias_msgs[-1].start()
    for q, ch in ((2, 1), (4, 0), (2, 0), (4, 1), (1, 0), (1, 1)):
        gate_up(q, ch).start()

    def expert_of(shape, dim):
        lane = lax.broadcasted_iota(jnp.int32, shape, dim)
        slot = lane & (SLOTS - 1)
        class_row = jnp.where(lane < SLOTS, row, row + away + RING)
        far = jnp.zeros_like(lane)
        side = jnp.zeros_like(lane)
        for m, (s, dc) in enumerate(ORDER):
            far = jnp.where(slot // 2 == m, 2 * s, far)
            side = jnp.where(slot // 2 == m, dc, side)
        expert = (((class_row + far) & (RING - 1)) * RING + ((col + side) & (RING - 1))) * 2 + jnp.where((slot & 1) == 1, 1 - core, core)
        return jnp.where(lane < 2 * SLOTS, expert, -1)

    n_exp = rw_v.shape[0]
    transposed = (((1,), (1,)), ((), ()))
    pick = jnp.where(expert_of((128, n_exp), 0) == lax.broadcasted_iota(jnp.int32, (128, n_exp), 1), 1.0, 0.0).astype(BF16)
    rwp_v[...] = jnp.dot(pick, rw_v[...], preferred_element_type=F32).astype(BF16)
    rb_p = lax.dot_general(jnp.broadcast_to(rb_v[...], (16, n_exp)), pick, transposed, preferred_element_type=F32)[0:1]
    expert = expert_of((1, 128), 1).astype(F32)
    load_x.wait()
    norm = norm_v[...].astype(F32)
    tn = tok // 4

    for i in range(4):
        rows = pl.ds(i * tn, tn)
        own = pl.ds(tok + i * tn, tn)
        xf = x_v[rows, :].astype(F32)
        inv = lax.rsqrt(jnp.mean(xf * xf, axis=-1, keepdims=True) + EPSILON)
        hidden = (xf * inv * norm).astype(BF16)
        h_v[own, :] = hidden
    hidden_send().start()
    for i in range(4):
        rows = pl.ds(i * tn, tn)
        own = pl.ds(tok + i * tn, tn)
        logits = lax.dot_general(h_v[own, :], rwp_v[...], transposed, preferred_element_type=F32) + rb_p
        ids = ids_v[:, i * tn:(i + 1) * tn].astype(F32).T
        chosen = ids[:, 0:1] == expert
        for e in range(1, top_k):
            chosen = chosen | (ids[:, e:e + 1] == expert)
        top = jnp.max(jnp.where(chosen, logits, -jnp.inf), axis=-1, keepdims=True)
        weight = jnp.where(chosen, jnp.exp(logits - top), 0.0)
        gates = weight / jnp.sum(weight, axis=-1, keepdims=True)
        g_v[own, :] = gates
        gsend[:, i * tn:(i + 1) * tn] = gates.T[SLOTS:2 * SLOTS]
    gates_send().start()
    for j in range(blocks):
        down(1, j).start()

    spans = [(0, lambda s: s // 2, lambda s: s % 2), (4, lambda s: s // 2, lambda s: s % 2),
             (8, lambda s: 2 + s, lambda s: 1 - s // 2), (12, lambda s: 2 + s, lambda s: s // 2),
             (16, lambda s: 6 + s, lambda s: 0), (18, lambda s: 8 + s // 2, lambda s: s % 2),
             (22, lambda s: 10 + s, lambda s: 1), (24, lambda s: 10 + s, lambda s: 0), (28, lambda s: 12 + s, lambda s: 1),
             (30, lambda s: 14 + s, lambda s: 1), (32, lambda s: 14 + s, lambda s: 0), (34, lambda s: 6 + s, lambda s: 1)]
    steps = 36

    def step_of(s):
        q, ch = 0, 0
        for at, q_at, ch_at in spans:
            r = jnp.maximum(s - at, 0)
            q = jnp.where(s >= at, q_at(r), q)
            ch = jnp.where(s >= at, ch_at(r), ch)
        return q, ch

    def buffer_of(s, q, ch):
        return jnp.where(q == 0, ch, 2 + lax.rem(s, 6))

    def weights_load(s):
        q, ch = step_of(s)
        b = buffer_of(s, q, ch)
        return pltpu.make_async_copy(wg.at[q, pl.ds(half_g * ch, half_g)], wbuf.at[pl.ds(half_g * b, half_g)], ld_sem.at[b])

    def landed(*msgs):
        for q, ch in msgs:
            gate_up(q, ch).wait_recv()

    def go(*msgs):
        for q, ch in msgs:
            gate_up(q, ch).start()

    def down_go(j, *qs):
        for q in qs:
            down(q, j).start()

    def down_landed(j, *qs):
        for q in qs:
            down(q, j).wait_recv()

    def down_relay_a(j):
        down_landed(j, 2, 4)
        for half in range(2):
            down(8, j, half).start()
        down_go(j, 3, 5)

    def down_relay_b(j):
        down_landed(j, 10, 12)
        for half in range(2):
            down(14, j, half).start()
        down_go(j, 11, 13)

    def event_3():
        hidden_send().wait_send()
        go((6, 0))
        hidden_send().wait_recv()

    def event_7():
        landed((2, 1), (4, 0))
        go((8, 1), (8, 0), (10, 1), (3, 1), (5, 0))

    def event_11():
        landed((2, 0), (4, 1))
        go((12, 1), (3, 0), (5, 1))

    def event_13():
        landed((6, 0))
        go((10, 0), (12, 0), (7, 0))
        down_go(0, 6)
        down_go(1, 6)
        go((6, 1))

    def event_17():
        down_go(0, 4)
        landed((8, 0), (8, 1))
        go((9, 0), (9, 1))
        down_go(2, 6)
        down_go(3, 6)

    def event_21():
        landed((10, 1))
        go((14, 1), (11, 1))
        down_go(0, 2)

    def event_23():
        landed((10, 0), (12, 0))
        go((14, 0), (11, 0), (13, 0))

    def event_27():
        landed((12, 1))
        go((13, 1))
        down_landed(0, 6)
        down_go(0, 10, 12, 7)
        down_go(1, 2, 4)

    def event_29():
        landed((14, 1))
        go((15, 1))

    def event_31():
        landed((14, 0))
        go((15, 0))
        down_relay_a(0)

    def event_33():
        landed((6, 1))
        go((7, 1))
        down_relay_b(0)
        for j in range(1, blocks):
            down_landed(j, 6)
            down_go(j, 7)
        down_go(1, 10, 12)
        down_go(2, 2, 4)

    events = {3: event_3, 7: event_7, 11: event_11, 13: event_13, 17: event_17, 21: event_21, 23: event_23, 27: event_27, 29: event_29, 31: event_31, 33: event_33}
    with scope('bias_wait'):
        for msg in bias_msgs:
            msg.wait_recv()

    @pl.loop(0, 8 + 2 * (steps - 8))
    def _(i):
        single = i < 8
        s = jnp.where(single, i, 4 + i // 2)
        q, ch = step_of(s)
        first = single | (lax.rem(i, 2) == 0)
        last = single | (lax.rem(i, 2) == 1)
        foreign = jnp.where(single, i // 4, lax.rem(i, 2))

        @pl.when(first & (q > 0))
        def _():
            with scope('load_wait'):
                weights_load(s).wait()

        @pl.when(last & (s < steps - 1))
        def _():
            @pl.when(lax.rem(s, 2) == 1)
            def _():
                for at, event in events.items():
                    @pl.when(s == at)
                    def _(event=event):
                        with scope(event.__name__):
                            event()

            q1, ch1 = step_of(s + 1)

            @pl.when((lax.rem(q1, 2) == 1) & ((s + 1 < 4) | (s + 1 >= 8)))
            def _():
                with scope('sib_wait'):
                    gate_up(q1, ch1).wait_recv()

            @pl.when(q1 > 0)
            def _():
                weights_load(s + 1).start()

        w_at = half_g * buffer_of(s, q, ch)
        bias_at = half_g * 2 * ch
        with scope('up'):
            for t in range(2):
                rows = pl.ds(pl.multiple_of((1 - foreign) * tok + t * tm, tm), tm)
                for g in range(half_g):
                    u = jnp.dot(h_v[rows, :], wbuf[w_at + g], preferred_element_type=F32)
                    a = (u[:, :128] + bias_v[q, pl.ds(bias_at + 2 * g, 1), :]).astype(BF16)
                    l = (u[:, 128:] + bias_v[q, pl.ds(bias_at + 2 * g + 1, 1), :]).astype(BF16)
                    a = jnp.minimum(a, LIMIT).astype(F32)
                    l = jnp.clip(l, -LIMIT, LIMIT).astype(F32)
                    z_v[q, rows, pl.ds(pl.multiple_of(128 * (half_g * ch + g), 128), 128)] = (a * jax.nn.sigmoid(ALPHA * a) * (l + 1.0)).astype(BF16)

    with scope('own_sent'):
        for q in (2, 4, 6, 1):
            for ch in range(2):
                gate_up(q, ch).wait_send()
    with scope('gates_in'):
        gates_send().wait_recv()
        for i in range(4):
            g_v[pl.ds(i * tn, tn), 0:SLOTS] = gfar[:, i * tn:(i + 1) * tn].T

    def down_load(j, q):
        spot = wbuf.at[SLOTS // 2 * lax.rem(j, 2) + q // 2, pl.ds(d_ff * (q % 2), d_ff)]
        src = wd_hbm.at[0, :, pl.ds(pl.multiple_of(j * COLS, COLS), COLS)] if q == 0 else wd.at[q, j]
        return pltpu.make_async_copy(src, spot, ld2_sem.at[lax.rem(j, 2), q])

    def relay(j):
        down_relay_a(j)
        down_relay_b(j)

        @pl.when(j + 1 < blocks)
        def _():
            down_go(j + 1, 10, 12)

        @pl.when(j + 2 < blocks)
        def _():
            down_go(j + 2, 2, 4)

    def load_early(j):
        for q in (0, 2, 4, 6, 10, 12):
            down_load(j, q).start()

    def load_sib(j):
        for q in (1, 3, 5, 7, 11, 13):
            down(q, j).wait_recv()
            down_load(j, q).start()

    def load_late(j):
        for q in relayed_slots:
            for half in range(2):
                down(q, j, half).wait_recv()
            down_go(j, q + 1)
            down_load(j, q).start()
        for q in relayed_slots:
            down(q + 1, j).wait_recv()
            down_load(j, q + 1).start()
        for q in range(SLOTS):
            down_load(j, q).wait()

    def out_copy(j, t):
        cols = pl.ds(pl.multiple_of(j * COLS, COLS), COLS)
        return pltpu.make_async_copy(ostage.at[t], out_hbm.at[pl.ds(t * tm, tm), cols], out_sem.at[t])

    def finish(j, wait_out):
        cols = pl.ds(pl.multiple_of(j * COLS, COLS), COLS)
        for t in range(2):
            sum_send(j, t).wait_recv()
            pl.when(wait_out)(lambda t=t: out_copy(j - 1, t).wait())
            total = acc[lax.rem(j, 2), 2 + t] + rs_v[j, t]
            ostage[t] = (x_v[pl.ds(t * tm, tm), cols].astype(F32) + total).astype(BF16)
            out_copy(j, t).start()

    load_early(0)
    load_sib(0)

    @pl.loop(0, blocks)
    def _(j):
        with scope('load_late'):
            load_late(j)
        par = lax.rem(j, 2)

        @pl.loop(0, 4)
        def _(t):
            @pl.when((t < 2) & (j >= 2))
            def _():
                sum_send(j - 2, t).wait_send()

            @pl.when((t == 1) & (j + 1 < blocks))
            def _():
                with scope('relay'):
                    relay(j + 1)
                    load_early(j + 1)

            @pl.when((t == 2) & (j + 1 < blocks))
            def _():
                with scope('load_sib'):
                    load_sib(j + 1)

            @pl.when((t == 3) & (j >= 1))
            def _():
                with scope('finish'):
                    finish(j - 1, j >= 2)

            rows = pl.ds(pl.multiple_of(t * tm, tm), tm)
            with scope('down'):
                total = None
                for e in range(SLOTS):
                    w = wbuf[SLOTS // 2 * par + e // 2, d_ff * (e % 2):d_ff * (e % 2 + 1), :]
                    y = jnp.dot(z_v[e, rows, :], w, preferred_element_type=F32)
                    b = jnp.concatenate([bias_v[e, pl.ds(2 * groups + 2 * j, 1), :], bias_v[e, pl.ds(2 * groups + 2 * j + 1, 1), :]], axis=1)
                    y = (y + b).astype(BF16).astype(F32)
                    p = g_v[rows, e:e + 1]
                    term = jnp.where(p > 0, y * p, 0.0)
                    total = term if total is None else total + term
                acc[par, t] = total

            @pl.when(t < 2)
            def _():
                sum_send(j, t).start()

    with scope('last_finish'):
        finish(blocks - 1, blocks >= 2)
        for t in range(2):
            out_copy(blocks - 1, t).wait()
    with scope('drain'):
        for t in range(2):
            for j in range(max(blocks - 2, 0), blocks):
                sum_send(j, t).wait_send()
        for q in range(SLOTS):
            for ch in range(2):
                if q not in (0, 1, 2, 4, 6):
                    gate_up(q, ch).wait_send()
            for j in range(blocks):
                if q in relayed_slots:
                    for half in range(2):
                        down(q, j, half).wait_send()
                elif q:
                    down(q, j).wait_send()
        for msg in bias_msgs:
            msg.wait_send()
        gates_send().wait_send()


def solution(mesh):
    rows_spec = P(('dp', 'ep'), None)
    assert mesh.shape['ep'] == 2 * RING * RING

    def local_block(x_in, expert_ids, norm_weight, router_w, router_b, w_gate_up, b_gate_up, w_down, b_down):
        tok, d_model = x_in.shape
        d_ff = w_down.shape[1]
        assert w_gate_up.shape[0] == 1 and tok >= d_model
        groups, blocks, tm = 2 * d_ff // COLS, d_model // COLS, tok // 2
        hbm = pl.BlockSpec(memory_space=pltpu.HBM)
        vmem = pl.BlockSpec(memory_space=pltpu.VMEM)
        dma = pltpu.SemaphoreType.DMA
        wide = max(groups * 4, SLOTS * d_ff // d_model * 2)
        out = pl.pallas_call(
            kernel,
            out_shape=(
                jax.ShapeDtypeStruct((tok, d_model), BF16),
                jax.ShapeDtypeStruct((SLOTS, groups, d_model, COLS), BF16),
                jax.ShapeDtypeStruct((SLOTS, blocks, d_ff, COLS), BF16),
            ),
            in_specs=[hbm, vmem, vmem, vmem, vmem, hbm, vmem, hbm, vmem],
            out_specs=(hbm, hbm, hbm),
            scratch_shapes=[
                pltpu.VMEM((SLOTS, 2 * tok, d_ff), BF16),
                pltpu.VMEM((2 * tok, d_model), BF16),
                pltpu.VMEM((wide, d_model, COLS), BF16),
                pltpu.VMEM((2 * tok, 128), F32),
                pltpu.VMEM((SLOTS, tok), F32),
                pltpu.VMEM((SLOTS, tok), F32),
                pltpu.VMEM((2, 4, tm, COLS), F32),
                pltpu.VMEM((blocks, 2, tm, COLS), F32),
                pltpu.VMEM((tok, d_model), BF16),
                pltpu.VMEM((2, tm, COLS), BF16),
                pltpu.VMEM((SLOTS, 2 * groups + d_model // 128, 128), F32),
                pltpu.VMEM((128, d_model), BF16),
                dma((SLOTS, 2)),
                dma((SLOTS, 2)),
                dma((SLOTS, blocks, 2)),
                dma((SLOTS, blocks, 2)),
                dma((SLOTS,)),
                dma((SLOTS,)),
                dma((2,)),
                dma((2,)),
                dma((blocks, 2)),
                dma((blocks, 2)),
                dma((8,)),
                dma((2, SLOTS)),
                dma((2,)),
                dma((2,)),
            ],
            compiler_params=pltpu.CompilerParams(collective_id=0, has_side_effects=True, vmem_limit_bytes=67043328),
        )(x_in, expert_ids.T, norm_weight[None], router_w.T, router_b[None], w_gate_up, b_gate_up, w_down, b_down)
        return out[0]

    return jax.shard_map(local_block, mesh=mesh, in_specs=(rows_spec, rows_spec, P(), P(), P(), P('ep', None, None), P('ep', None), P('ep', None, None), P('ep', None)), out_specs=rows_spec, check_vma=False)
```

time: 266 us -> 230 us (0.86)
  Pallas kernels: 257 us -> 225 us
  local copies, waits for them, and re-layouts: 7.79 us -> 4.36 us
    pallas_call x1, Pallas kernels: 257 us -> 225 us  [local_block(): pl.pallas_call(kernel, out_shape=(jax.ShapeDtypeStruct((tok, d_model), BF...]
    unnamed x3 -> x1, local copies, waits for them, and re-layouts: 6.51 us -> 3.08 us
where the time goes in v2:
time: 230 us
  Pallas kernels  225 us (98%)
  local copies, waits for them, and re-layouts  4.36 us (2%)
    pallas_call x1, Pallas kernels, local_block(): pl.pallas_call(kernel, out_shape=(jax.ShapeDtypeStruct((tok, d_model), BF...  225 us

profile of v2, /device:TPU:97, one launch (start us, length us, event | category | flops | bytes accessed | tf_op | source)
XLA Modules:
  0.0 229.6 jit_solution(8468677967907843468)
XLA Ops:
  0.0 1.3 broadcast_in_dim.6.norm_v
  1.3 225.3 %shard_map.91 = (bf16[1024,1024]{1,0:T(8,128)(2,1)}, bf16[16,4,1024,256]{3,2,1,0:T(8,128)(2,1)}, bf16[16,4,512,256]{3,2,1,0:T(8,128)(2,1)}) custom-call(bf16[1024,1024]{1,0:T(8,128)(2,1)} %x_hbm.1, s32[8,1024]{1,0:T(8,128)} %bitcast.4, bf16[1,1024]{1,0:T(2,128)(2,1)} %broadcast_in_dim.6.norm_v, bf16[32,1024]{1,0:T(8,128)(2,1)} %bitcast.3, ...), custom_call_target="tpu_custom_call" | custom-call | tf_op jit(solution)/shard_map/pallas_call | solution.py:471
  226.6 3.1 %copy.11 = bf16[1024,1024]{1,0:T(8,128)(2,1)} copy(bf16[1024,1024]{1,0:T(8,128)(2,1)} %get-tuple-element.6) | data formatting | bytes 4194304

commit v3 on v2

--- a/solution.py
+++ b/solution.py
@@ -14,9 +14,47 @@
 RING = 4
 ORDER = [(0, 0), (0, 3), (0, 1), (1, 0), (0, 2), (1, 3), (1, 1), (1, 2)]
 SLOTS = 2 * len(ORDER)
-
-
-def kernel(x_hbm, ids_v, norm_v, rw_v, rb_v, wgu_hbm, bgu_v, wd_hbm, bd_v, out_hbm, wg, wd, z_v, h_v, wbuf, g_v, gfar, gsend, acc, rs_v, x_v, ostage, bias_v, rwp_v, wg_s, wg_r, wd_s, wd_r, bias_s, bias_r, hg_s, hg_r, rs_s, rs_r, ld_sem, ld2_sem, in_sem, out_sem):
+NAMES = 'aAbBcCdDeEfFgGhH'
+GATE_UP_WAYS = 'b0a+,b1a+,c0a-,c1a-,d0ay,d1ay,e0c-,e1b+,' + 'f0d+,f1by,g0d-,g1cy,h0g-,h1f+'
+DOWN_WAYS = 'b.a+,c.a-,d.ay,e0b+,e1c-,f.d+,g.d-,h0f+,h1g-'
+STEPS = 'a0a1A0A1a0a1A0A1b1B1c0C0b0B0c1C1d0D0' + 'e0e1E0E1f1F1f0F0g0G0g1G1h1H1h0H0d1D1'
+PHASE_1 = {
+    3: ['~,!d0,?~'],
+    7: ['?b1,?c0,!e1,!e0,!f1,!B1,!C0'],
+    11: ['?b0,?c1,!g1,!B0,!C1'],
+    13: ['?d0,!f0,!g0,!D0,!d.0,!d1'],
+    17: ['!c.0,?e0,?e1,!E0,!E1,!d.1,!d.2,!d.3'],
+    21: ['?f1,!h1,!F1,!b.0'],
+    23: ['?f0,?g0,!h0,!F0,!G0'],
+    27: ['?g1,!G1,?d.0,!f.0,!g.0,!D.0,!b.1,!c.1'],
+    29: ['?h1,!H1'],
+    31: ['?h0,!H0', 'r0'],
+    33: ['s0,?d1,!D1,?d.1,!f.1,!g.1,!b.2,!c.2,!D.1'],
+}
+PHASE_2 = {
+    0: ['i0,j0,k0,l0,w0'],
+    1: ['r1,s1,?d.2,!f.2,!g.2,!b.3,!c.3,!D.2,i1'],
+    2: ['j1'],
+    4: ['k1,l1,w1'],
+    5: ['r2,s2,?d.3,!f.3,!g.3,!D.3,i2'],
+    6: ['j2'],
+    7: ['r3'],
+    8: ['k2,l2,w2'],
+    9: ['s3,i3'],
+    10: ['j3'],
+    12: ['k3,l3,w3'],
+}
+SHORT = {'r': '?b,?c,!e,!B,!C', 's': '?f,?g,!h,!F,!G', 'i': '<a,<b,<c,<d,<f,<g', 'j': '?A,<A,?B,<B,?C,<C,?D,<D,?F,<F,?G,<G',
+         'k': '?e,!E,<e,?h,!H,<h', 'l': '?E,<E,?H,<H'}
+
+
+def kernel(*refs):
+    slots, blocks = refs[10].shape[0], refs[11].shape[1]
+    counts = [(slots, 2), (slots, 2), (slots, blocks, 2), (slots, blocks, 2), (slots,), (slots,), (2,), (2,), (blocks, 2), (blocks, 2), (8,), (2, slots), (2,), (2,)]
+    pl.run_scoped(lambda *sems: body(*refs, *sems), *[pltpu.SemaphoreType.DMA(c) for c in counts])
+
+
+def body(x_hbm, ids_v, norm_v, rw_v, rb_v, wgu_hbm, bgu_v, wd_hbm, bd_v, out_hbm, wg, wd, z_v, h_v, wbuf, g_v, gfar, gsend, acc, rs_v, x_v, ostage, bias_v, rwp_v, wg_s, wg_r, wd_s, wd_r, bias_s, bias_r, hg_s, hg_r, rs_s, rs_r, ld_sem, ld2_sem, in_sem, out_sem):
     tok, d_model = x_hbm.shape
     d_ff = wd_hbm.shape[1]
     groups = 2 * d_ff // COLS
@@ -42,31 +80,33 @@
     def remote(src, dst, ssem, rsem, where):
         return pltpu.make_async_remote_copy(src_ref=src, dst_ref=dst, send_sem=ssem, recv_sem=rsem, device_id=where, device_id_type=MESH)
 
-    gate_up_way = {(2, 0): (0, 1), (2, 1): (0, 1), (4, 0): (0, -1), (4, 1): (0, -1), (6, 0): (0, 'y'), (6, 1): (0, 'y'), (8, 0): (4, -1), (8, 1): (2, 1),
-                   (10, 0): (6, 1), (10, 1): (2, 'y'), (12, 0): (6, -1), (12, 1): (4, 'y'), (14, 0): (12, -1), (14, 1): (10, 1)}
-    down_way = {2: (0, 1), 4: (0, -1), 6: (0, 'y'), (8, 0): (2, 1), (8, 1): (4, -1), 10: (6, 1), 12: (6, -1), (14, 0): (10, 1), (14, 1): (12, -1)}
-    relayed_slots = (8, 14)
+    def ways(table):
+        return {(NAMES.index(m[0]), m[1]): (NAMES.index(m[2]), m[3]) for m in table.split(',')}
+
+    gate_up_way, down_way = ways(GATE_UP_WAYS), ways(DOWN_WAYS)
+    relayed_slots = [NAMES.index(n) for n in 'eh']
 
     def target(way):
-        if way == 'sib':
+        if way == 's':
             return dev(0, 0, 1)
-        return dev(2, 0) if way == 'y' else dev(0, way)
+        return dev(2, 0) if way == 'y' else dev(0, 1 if way == '+' else -1)
 
     def gate_up(q, ch):
-        src, way = gate_up_way.get((q, ch), (None, 'sib')) if isinstance(q, int) else (None, 'sib')
+        static = isinstance(q, int)
+        src, way = gate_up_way.get((q, str(ch)), (q - 1, 's')) if static else (q - 1, 's')
         part = pl.ds(half_g * ch, half_g)
-        if src == 0 or (isinstance(q, int) and q == 1):
-            here = wbuf.at[part]
-        else:
-            here = wg.at[q - 1 if src is None else src, part]
+        here = wbuf.at[part] if static and src == 0 else wg.at[src, part]
         return remote(here, wg.at[q, part], wg_s.at[q, ch], wg_r.at[q, ch], target(way))
 
-    def down(q, j, half=None):
-        src, way = down_way.get(q if half is None else (q, half), (q - 1, 'sib'))
-        rows = slice(None) if half is None else pl.ds(d_ff // 2 * half, d_ff // 2)
-        here = wd_hbm.at[0, :, pl.ds(pl.multiple_of(j * COLS, COLS), COLS)] if src == 0 else wd.at[src, j, rows]
-        at = 0 if half is None else half
-        return remote(here, wd.at[q, j, rows], wd_s.at[q, j, at], wd_r.at[q, j, at], target(way))
+    def down(q, j):
+        def one(half):
+            src, way = down_way.get((q, half), (q - 1, 's'))
+            rows = slice(None) if half == '.' else pl.ds(d_ff // 2 * int(half), d_ff // 2)
+            here = wd_hbm.at[0, :, pl.ds(j * COLS, COLS)] if src == 0 else wd.at[src, j, rows]
+            at = 0 if half == '.' else int(half)
+            return remote(here, wd.at[q, j, rows], wd_s.at[q, j, at], wd_r.at[q, j, at], target(way))
+
+        return [one(half) for half in ('01' if q in relayed_slots else '.')]
 
     def hidden_send():
         return remote(h_v.at[pl.ds(tok, tok)], h_v.at[pl.ds(0, tok)], hg_s.at[0], hg_r.at[0], dev(away, 0))
@@ -108,8 +148,8 @@
             if q:
                 bias_msgs.append(bias_send(q, dev(2 * s, dc, f)))
                 bias_msgs[-1].start()
-    for q, ch in ((2, 1), (4, 0), (2, 0), (4, 1), (1, 0), (1, 1)):
-        gate_up(q, ch).start()
+    for name in 'b1,c0,b0,c1,A0,A1'.split(','):
+        gate_up(NAMES.index(name[0]), int(name[1])).start()
 
     def expert_of(shape, dim):
         lane = lax.broadcasted_iota(jnp.int32, shape, dim)
@@ -130,7 +170,7 @@
     rb_p = lax.dot_general(jnp.broadcast_to(rb_v[...], (16, n_exp)), pick, transposed, preferred_element_type=F32)[0:1]
     expert = expert_of((1, 128), 1).astype(F32)
     load_x.wait()
-    norm = norm_v[...].astype(F32)
+    norm = jnp.concatenate([norm_v[i:i + 1, :].astype(F32) for i in range(d_model // 128)], axis=1)
     tn = tok // 4
 
     for i in range(4):
@@ -156,22 +196,20 @@
         gsend[:, i * tn:(i + 1) * tn] = gates.T[SLOTS:2 * SLOTS]
     gates_send().start()
     for j in range(blocks):
-        down(1, j).start()
-
-    spans = [(0, lambda s: s // 2, lambda s: s % 2), (4, lambda s: s // 2, lambda s: s % 2),
-             (8, lambda s: 2 + s, lambda s: 1 - s // 2), (12, lambda s: 2 + s, lambda s: s // 2),
-             (16, lambda s: 6 + s, lambda s: 0), (18, lambda s: 8 + s // 2, lambda s: s % 2),
-             (22, lambda s: 10 + s, lambda s: 1), (24, lambda s: 10 + s, lambda s: 0), (28, lambda s: 12 + s, lambda s: 1),
-             (30, lambda s: 14 + s, lambda s: 1), (32, lambda s: 14 + s, lambda s: 0), (34, lambda s: 6 + s, lambda s: 1)]
-    steps = 36
+        for msg in down(1, j):
+            msg.start()
+
+    codes = [2 * NAMES.index(n) + int(ch) for n, ch in zip(STEPS[::2], STEPS[1::2])]
+    steps = len(codes)
+    per, bits = 6, 5
+    words = [sum(c << bits * i for i, c in enumerate(codes[at:at + per])) for at in range(0, steps, per)]
 
     def step_of(s):
-        q, ch = 0, 0
-        for at, q_at, ch_at in spans:
-            r = jnp.maximum(s - at, 0)
-            q = jnp.where(s >= at, q_at(r), q)
-            ch = jnp.where(s >= at, ch_at(r), ch)
-        return q, ch
+        word = jnp.int32(words[0])
+        for i, w in enumerate(words[1:]):
+            word = jnp.where(s >= per * (i + 1), w, word)
+        code = lax.shift_right_logical(word, bits * lax.rem(s, per)) & ((1 << bits) - 1)
+        return code // 2, lax.rem(code, 2)
 
     def buffer_of(s, q, ch):
         return jnp.where(q == 0, ch, 2 + lax.rem(s, 6))
@@ -181,97 +219,43 @@
         b = buffer_of(s, q, ch)
         return pltpu.make_async_copy(wg.at[q, pl.ds(half_g * ch, half_g)], wbuf.at[pl.ds(half_g * b, half_g)], ld_sem.at[b])
 
-    def landed(*msgs):
-        for q, ch in msgs:
-            gate_up(q, ch).wait_recv()
-
-    def go(*msgs):
-        for q, ch in msgs:
-            gate_up(q, ch).start()
-
-    def down_go(j, *qs):
-        for q in qs:
-            down(q, j).start()
-
-    def down_landed(j, *qs):
-        for q in qs:
-            down(q, j).wait_recv()
-
-    def down_relay_a(j):
-        down_landed(j, 2, 4)
-        for half in range(2):
-            down(8, j, half).start()
-        down_go(j, 3, 5)
-
-    def down_relay_b(j):
-        down_landed(j, 10, 12)
-        for half in range(2):
-            down(14, j, half).start()
-        down_go(j, 11, 13)
-
-    def event_3():
-        hidden_send().wait_send()
-        go((6, 0))
-        hidden_send().wait_recv()
-
-    def event_7():
-        landed((2, 1), (4, 0))
-        go((8, 1), (8, 0), (10, 1), (3, 1), (5, 0))
-
-    def event_11():
-        landed((2, 0), (4, 1))
-        go((12, 1), (3, 0), (5, 1))
-
-    def event_13():
-        landed((6, 0))
-        go((10, 0), (12, 0), (7, 0))
-        down_go(0, 6)
-        down_go(1, 6)
-        go((6, 1))
-
-    def event_17():
-        down_go(0, 4)
-        landed((8, 0), (8, 1))
-        go((9, 0), (9, 1))
-        down_go(2, 6)
-        down_go(3, 6)
-
-    def event_21():
-        landed((10, 1))
-        go((14, 1), (11, 1))
-        down_go(0, 2)
-
-    def event_23():
-        landed((10, 0), (12, 0))
-        go((14, 0), (11, 0), (13, 0))
-
-    def event_27():
-        landed((12, 1))
-        go((13, 1))
-        down_landed(0, 6)
-        down_go(0, 10, 12, 7)
-        down_go(1, 2, 4)
-
-    def event_29():
-        landed((14, 1))
-        go((15, 1))
-
-    def event_31():
-        landed((14, 0))
-        go((15, 0))
-        down_relay_a(0)
-
-    def event_33():
-        landed((6, 1))
-        go((7, 1))
-        down_relay_b(0)
-        for j in range(1, blocks):
-            down_landed(j, 6)
-            down_go(j, 7)
-        down_go(1, 10, 12)
-        down_go(2, 2, 4)
-
-    events = {3: event_3, 7: event_7, 11: event_11, 13: event_13, 17: event_17, 21: event_21, 23: event_23, 27: event_27, 29: event_29, 31: event_31, 33: event_33}
+    def down_load(j, q):
+        spot = wbuf.at[SLOTS // 2 * (j % 2) + q // 2, pl.ds(d_ff * (q % 2), d_ff)]
+        src = wd_hbm.at[0, :, pl.ds(j * COLS, COLS)] if q == 0 else wd.at[q, j]
+        return pltpu.make_async_copy(src, spot, ld2_sem.at[j % 2, q])
+
+    def act(text):
+        for word in text.split(','):
+            what, name, rest = word[0], word[1:2], word[2:]
+            if what == '~':
+                hidden_send().wait_send()
+            elif name == '~':
+                hidden_send().wait_recv()
+            elif what == 'w':
+                for q in range(SLOTS):
+                    down_load(int(name), q).wait()
+            elif what in SHORT:
+                if int(name) < blocks:
+                    act(','.join(w + '.' + name for w in SHORT[what].split(',')))
+            elif rest[0] != '.':
+                msg = gate_up(NAMES.index(name), int(rest))
+                msg.start() if what == '!' else msg.wait_recv()
+            elif int(rest[1:]) < blocks:
+                q, j = NAMES.index(name), int(rest[1:])
+                if what == '<':
+                    down_load(j, q).start()
+                else:
+                    for msg in down(q, j):
+                        msg.start() if what == '!' else msg.wait_recv()
+
+    def events(table, now):
+        for at, texts in table.items():
+            @pl.when(now == at)
+            def _(at=at, texts=texts):
+                with scope('event_' + str(at)):
+                    for text in texts:
+                        act(text)
+
     with scope('bias_wait'):
         for msg in bias_msgs:
             msg.wait_recv()
@@ -294,15 +278,11 @@
         def _():
             @pl.when(lax.rem(s, 2) == 1)
             def _():
-                for at, event in events.items():
-                    @pl.when(s == at)
-                    def _(event=event):
-                        with scope(event.__name__):
-                            event()
+                events(PHASE_1, s)
 
             q1, ch1 = step_of(s + 1)
 
-            @pl.when((lax.rem(q1, 2) == 1) & ((s + 1 < 4) | (s + 1 >= 8)))
+            @pl.when((lax.rem(q1, 2) == 1) & ((s < 3) | (s >= 7)))
             def _():
                 with scope('sib_wait'):
                     gate_up(q1, ch1).wait_recv()
@@ -333,44 +313,6 @@
         for i in range(4):
             g_v[pl.ds(i * tn, tn), 0:SLOTS] = gfar[:, i * tn:(i + 1) * tn].T
 
-    def down_load(j, q):
-        spot = wbuf.at[SLOTS // 2 * lax.rem(j, 2) + q // 2, pl.ds(d_ff * (q % 2), d_ff)]
-        src = wd_hbm.at[0, :, pl.ds(pl.multiple_of(j * COLS, COLS), COLS)] if q == 0 else wd.at[q, j]
-        return pltpu.make_async_copy(src, spot, ld2_sem.at[lax.rem(j, 2), q])
-
-    def relay(j):
-        down_relay_a(j)
-        down_relay_b(j)
-
-        @pl.when(j + 1 < blocks)
-        def _():
-            down_go(j + 1, 10, 12)
-
-        @pl.when(j + 2 < blocks)
-        def _():
-            down_go(j + 2, 2, 4)
-
-    def load_early(j):
-        for q in (0, 2, 4, 6, 10, 12):
-            down_load(j, q).start()
-
-    def load_sib(j):
-        for q in (1, 3, 5, 7, 11, 13):
-            down(q, j).wait_recv()
-            down_load(j, q).start()
-
-    def load_late(j):
-        for q in relayed_slots:
-            for half in range(2):
-                down(q, j, half).wait_recv()
-            down_go(j, q + 1)
-            down_load(j, q).start()
-        for q in relayed_slots:
-            down(q + 1, j).wait_recv()
-            down_load(j, q + 1).start()
-        for q in range(SLOTS):
-            down_load(j, q).wait()
-
     def out_copy(j, t):
         cols = pl.ds(pl.multiple_of(j * COLS, COLS), COLS)
         return pltpu.make_async_copy(ostage.at[t], out_hbm.at[pl.ds(t * tm, tm), cols], out_sem.at[t])
@@ -384,13 +326,8 @@
             ostage[t] = (x_v[pl.ds(t * tm, tm), cols].astype(F32) + total).astype(BF16)
             out_copy(j, t).start()
 
-    load_early(0)
-    load_sib(0)
-
     @pl.loop(0, blocks)
     def _(j):
-        with scope('load_late'):
-            load_late(j)
         par = lax.rem(j, 2)
 
         @pl.loop(0, 4)
@@ -399,16 +336,7 @@
             def _():
                 sum_send(j - 2, t).wait_send()
 
-            @pl.when((t == 1) & (j + 1 < blocks))
-            def _():
-                with scope('relay'):
-                    relay(j + 1)
-                    load_early(j + 1)
-
-            @pl.when((t == 2) & (j + 1 < blocks))
-            def _():
-                with scope('load_sib'):
-                    load_sib(j + 1)
+            events({at: texts for at, texts in PHASE_2.items() if at < 4 * blocks}, 4 * j + t)
 
             @pl.when((t == 3) & (j >= 1))
             def _():
@@ -444,12 +372,9 @@
             for ch in range(2):
                 if q not in (0, 1, 2, 4, 6):
                     gate_up(q, ch).wait_send()
-            for j in range(blocks):
-                if q in relayed_slots:
-                    for half in range(2):
-                        down(q, j, half).wait_send()
-                elif q:
-                    down(q, j).wait_send()
+            for j in range(blocks if q else 0):
+                for msg in down(q, j):
+                    msg.wait_send()
         for msg in bias_msgs:
             msg.wait_send()
         gates_send().wait_send()
@@ -466,7 +391,6 @@
         groups, blocks, tm = 2 * d_ff // COLS, d_model // COLS, tok // 2
         hbm = pl.BlockSpec(memory_space=pltpu.HBM)
         vmem = pl.BlockSpec(memory_space=pltpu.VMEM)
-        dma = pltpu.SemaphoreType.DMA
         wide = max(groups * 4, SLOTS * d_ff // d_model * 2)
         out = pl.pallas_call(
             kernel,
@@ -490,23 +414,9 @@
                 pltpu.VMEM((2, tm, COLS), BF16),
                 pltpu.VMEM((SLOTS, 2 * groups + d_model // 128, 128), F32),
                 pltpu.VMEM((128, d_model), BF16),
-                dma((SLOTS, 2)),
-                dma((SLOTS, 2)),
-                dma((SLOTS, blocks, 2)),
-                dma((SLOTS, blocks, 2)),
-                dma((SLOTS,)),
-                dma((SLOTS,)),
-                dma((2,)),
-                dma((2,)),
-                dma((blocks, 2)),
-                dma((blocks, 2)),
-                dma((8,)),
-                dma((2, SLOTS)),
-                dma((2,)),
-                dma((2,)),
             ],
             compiler_params=pltpu.CompilerParams(collective_id=0, has_side_effects=True, vmem_limit_bytes=67043328),
-        )(x_in, expert_ids.T, norm_weight[None], router_w.T, router_b[None], w_gate_up, b_gate_up, w_down, b_down)
+        )(x_in, expert_ids.T, norm_weight.reshape(-1, 128), router_w.T, router_b[None], w_gate_up, b_gate_up, w_down, b_down)
         return out[0]
 
     return jax.shard_map(local_block, mesh=mesh, in_specs=(rows_spec, rows_spec, P(), P(), P(), P('ep', None, None), P('ep', None), P('ep', None, None), P('ep', None)), out_specs=rows_spec, check_vma=False)

time: 230 us -> 219 us (0.952)
  Pallas kernels: 225 us -> 216 us
    pallas_call x1, Pallas kernels: 225 us -> 216 us  [local_block(): pl.pallas_call(kernel, out_shape=(jax.ShapeDtypeStruct((tok, d_model), BF...]
where the time goes in v3:
time: 219 us
  Pallas kernels  216 us (99%)
  local copies, waits for them, and re-layouts  3.08 us (1%)
    pallas_call x1, Pallas kernels, local_block(): pl.pallas_call(kernel, out_shape=(jax.ShapeDtypeStruct((tok, d_model), BF...  216 us

profile of v3, /device:TPU:97, one launch (start us, length us, event | category | flops | bytes accessed | tf_op | source)
XLA Modules:
  0.0 219.1 jit_solution(2727110700644278477)
XLA Ops:
  0.0 216.0 %shard_map.91 = (bf16[1024,1024]{1,0:T(8,128)(2,1)}, bf16[16,4,1024,256]{3,2,1,0:T(8,128)(2,1)}, bf16[16,4,512,256]{3,2,1,0:T(8,128)(2,1)}) custom-call(bf16[1024,1024]{1,0:T(8,128)(2,1)} %refs_0_.1, s32[8,1024]{1,0:T(8,128)} %bitcast.5, bf16[8,128]{1,0:T(8,128)(2,1)} %bitcast.6, bf16[32,1024]{1,0:T(8,128)(2,1)} %bitcast.4, bf16[1,32]{1,0:T(2,128)(2,1)} %bitcast.7, ...), custom_call_target="tpu_custom_call" | custom-call | tf_op jit(solution)/shard_map/pallas_call | solution.py:395
  216.0 3.1 %copy.11 = bf16[1024,1024]{1,0:T(8,128)(2,1)} copy(bf16[1024,1024]{1,0:T(8,128)(2,1)} %get-tuple-element.6) | data formatting | bytes 4194304

commit v4 on v3

--- a/solution.py
+++ b/solution.py
@@ -14,34 +14,39 @@
 RING = 4
 ORDER = [(0, 0), (0, 3), (0, 1), (1, 0), (0, 2), (1, 3), (1, 1), (1, 2)]
 SLOTS = 2 * len(ORDER)
+SCRATCH = 18
 NAMES = 'aAbBcCdDeEfFgGhH'
 GATE_UP_WAYS = 'b0a+,b1a+,c0a-,c1a-,d0ay,d1ay,e0c-,e1b+,' + 'f0d+,f1by,g0d-,g1cy,h0g-,h1f+'
 DOWN_WAYS = 'b.a+,c.a-,d.ay,e0b+,e1c-,f.d+,g.d-,h0f+,h1g-'
+FIRST_WAYS = 'h0ey,h1ey'
 STEPS = 'a0a1A0A1a0a1A0A1b1B1c0C0b0B0c1C1d0D0' + 'e0e1E0E1f1F1f0F0g0G0g1G1h1H1h0H0d1D1'
 PHASE_1 = {
     3: ['~,!d0,?~'],
     7: ['?b1,?c0,!e1,!e0,!f1,!B1,!C0'],
     11: ['?b0,?c1,!g1,!B0,!C1'],
     13: ['?d0,!f0,!g0,!D0,!d.0,!d1'],
-    17: ['!c.0,?e0,?e1,!E0,!E1,!d.1,!d.2,!d.3'],
+    17: ['!c.0,?e0,?e1,!E0,!E1,!d.1'],
     21: ['?f1,!h1,!F1,!b.0'],
     23: ['?f0,?g0,!h0,!F0,!G0'],
-    27: ['?g1,!G1,?d.0,!f.0,!g.0,!D.0,!b.1,!c.1'],
+    27: ['?g1,!G1,?d.0,!f.0,!g.0,!D.0'],
     29: ['?h1,!H1'],
-    31: ['?h0,!H0', 'r0'],
-    33: ['s0,?d1,!D1,?d.1,!f.1,!g.1,!b.2,!c.2,!D.1'],
+    31: ['?h0,!H0', 'r0,!b.1,!c.1'],
+    33: ['?d1,!D1,?d.1,!f.1,!g.1,!D.1', '?f.0,?g.0,!F.0,!G.0'],
+    34: ['?e.0,!h.0,!E.0,!d.2,!d.3,!b.2,!c.2'],
 }
 PHASE_2 = {
-    0: ['i0,j0,k0,l0,w0'],
-    1: ['r1,s1,?d.2,!f.2,!g.2,!b.3,!c.3,!D.2,i1'],
-    2: ['j1'],
-    4: ['k1,l1,w1'],
-    5: ['r2,s2,?d.3,!f.3,!g.3,!D.3,i2'],
+    0: ['i0,j0,<e.0,r1,?h.0,!H.0,<h.0,s1,l0,w0'],
+    1: ['i1'],
+    2: ['?d.2,!f.2,!g.2,!D.2,r2,j1'],
+    3: ['k1'],
+    4: ['l1,w1'],
+    5: ['s2,!b.3,!c.3,?d.3,!f.3,!g.3,!D.3,i2'],
     6: ['j2'],
-    7: ['r3'],
-    8: ['k2,l2,w2'],
-    9: ['s3,i3'],
-    10: ['j3'],
+    7: ['k2'],
+    8: ['l2,w2'],
+    9: ['r3'],
+    10: ['s3,i3'],
+    11: ['j3'],
     12: ['k3,l3,w3'],
 }
 SHORT = {'r': '?b,?c,!e,!B,!C', 's': '?f,?g,!h,!F,!G', 'i': '<a,<b,<c,<d,<f,<g', 'j': '?A,<A,?B,<B,?C,<C,?D,<D,?F,<F,?G,<G',
@@ -49,19 +54,20 @@
 
 
 def kernel(*refs):
-    slots, blocks = refs[10].shape[0], refs[11].shape[1]
-    counts = [(slots, 2), (slots, 2), (slots, blocks, 2), (slots, blocks, 2), (slots,), (slots,), (2,), (2,), (blocks, 2), (blocks, 2), (8,), (2, slots), (2,), (2,)]
+    wd = refs[len(refs) - SCRATCH - 1]
+    slots, blocks = wd.shape[:2]
+    counts = [(slots, 2), (slots, 2), (slots, blocks, 2), (slots, blocks, 2), (slots,), (slots,), (2,), (2,), (blocks, 4), (blocks, 4), (8,), (2, slots), (8,), (2,)]
     pl.run_scoped(lambda *sems: body(*refs, *sems), *[pltpu.SemaphoreType.DMA(c) for c in counts])
 
 
-def body(x_hbm, ids_v, norm_v, rw_v, rb_v, wgu_hbm, bgu_v, wd_hbm, bd_v, out_hbm, wg, wd, z_v, h_v, wbuf, g_v, gfar, gsend, acc, rs_v, x_v, ostage, bias_v, rwp_v, wg_s, wg_r, wd_s, wd_r, bias_s, bias_r, hg_s, hg_r, rs_s, rs_r, ld_sem, ld2_sem, in_sem, out_sem):
+def body(x_hbm, ids_hbm, norm_hbm, rw_hbm, rb_hbm, wgu_hbm, bgu_hbm, wd_hbm, bd_hbm, out_hbm, wg, wd, z_v, h_v, wbuf, g_v, gfar, gsend, acc, rs_v, x_v, ostage, bias_v, rwp_v, ids_v, norm_v, rw_v, rb_v, bgu_v, bd_v, wg_s, wg_r, wd_s, wd_r, bias_s, bias_r, hg_s, hg_r, rs_s, rs_r, ld_sem, ld2_sem, in_sem, out_sem):
     tok, d_model = x_hbm.shape
     d_ff = wd_hbm.shape[1]
     groups = 2 * d_ff // COLS
     half_g = groups // 2
     blocks = d_model // COLS
     tm = tok // 2
-    top_k = ids_v.shape[0]
+    top_k = ids_hbm.shape[0]
     me = lax.axis_index('ep')
     core = lax.rem(me, 2)
     col = lax.rem(me // 2, RING)
@@ -83,7 +89,7 @@
     def ways(table):
         return {(NAMES.index(m[0]), m[1]): (NAMES.index(m[2]), m[3]) for m in table.split(',')}
 
-    gate_up_way, down_way = ways(GATE_UP_WAYS), ways(DOWN_WAYS)
+    gate_up_way, down_way, first_way = ways(GATE_UP_WAYS), ways(DOWN_WAYS), ways(FIRST_WAYS)
     relayed_slots = [NAMES.index(n) for n in 'eh']
 
     def target(way):
@@ -101,6 +107,8 @@
     def down(q, j):
         def one(half):
             src, way = down_way.get((q, half), (q - 1, 's'))
+            if j == 0:
+                src, way = first_way.get((q, half), (src, way))
             rows = slice(None) if half == '.' else pl.ds(d_ff // 2 * int(half), d_ff // 2)
             here = wd_hbm.at[0, :, pl.ds(j * COLS, COLS)] if src == 0 else wd.at[src, j, rows]
             at = 0 if half == '.' else int(half)
@@ -120,15 +128,20 @@
     def sum_send(j, t):
         return remote(acc.at[lax.rem(j, 2), t], rs_v.at[j, t], rs_s.at[j, t], rs_r.at[j, t], dev(-away, 0))
 
+    def last_sum_send(i):
+        j, t, rows = blocks - 1, i // 2, pl.ds(pl.multiple_of(tm // 2 * lax.rem(i, 2), tm // 2), tm // 2)
+        return remote(acc.at[j % 2, t, rows], rs_v.at[j, t, rows], rs_s.at[j, i], rs_r.at[j, i], dev(-away, 0))
+
     raw = h_v.at[pl.ds(tok, tok)]
-    load_w = pltpu.make_async_copy(wgu_hbm.at[0], raw.at[pl.ds(0, d_model)], in_sem.at[0])
-    load_x = pltpu.make_async_copy(x_hbm, x_v, in_sem.at[1])
-    load_w.start()
-    load_x.start()
-
+    ins = [(wgu_hbm.at[0], raw.at[pl.ds(0, d_model)]), (bgu_hbm, bgu_v), (bd_hbm, bd_v), (x_hbm, x_v), (rw_hbm, rw_v), (rb_hbm, rb_v), (ids_hbm, ids_v), (norm_hbm, norm_v)]
+    loads = [pltpu.make_async_copy(src, dst, in_sem.at[i]) for i, (src, dst) in enumerate(ins)]
+    for load in loads:
+        load.start()
     ri = lax.broadcasted_iota(jnp.int32, (COLS, COLS), 0)
     ci = lax.broadcasted_iota(jnp.int32, (COLS, COLS), 1)
     split = jnp.where(ri == jnp.where(ci < COLS // 2, 2 * ci, 2 * ci - (COLS - 1)), 1.0, 0.0).astype(BF16)
+    for load in loads[1:3]:
+        load.wait()
     for g in range(groups):
         b = jnp.dot(jnp.broadcast_to(bgu_v[:, COLS * g:COLS * (g + 1)], (16, COLS)), split, preferred_element_type=F32)
         bias_v[0, 2 * g:2 * g + 1, :] = b[0:1, :128]
@@ -136,7 +149,7 @@
     for i in range(d_model // 128):
         bias_v[0, 2 * groups + i:2 * groups + i + 1, :] = bd_v[:, 128 * i:128 * (i + 1)].astype(F32)
     with scope('load_w'):
-        load_w.wait()
+        loads[0].wait()
     for g in range(groups):
         wbuf[g] = jnp.dot(raw[pl.ds(0, d_model), COLS * g:COLS * (g + 1)], split, preferred_element_type=F32).astype(BF16)
     with scope('barrier'):
@@ -163,13 +176,14 @@
         expert = (((class_row + far) & (RING - 1)) * RING + ((col + side) & (RING - 1))) * 2 + jnp.where((slot & 1) == 1, 1 - core, core)
         return jnp.where(lane < 2 * SLOTS, expert, -1)
 
+    for load in loads[3:]:
+        load.wait()
     n_exp = rw_v.shape[0]
     transposed = (((1,), (1,)), ((), ()))
     pick = jnp.where(expert_of((128, n_exp), 0) == lax.broadcasted_iota(jnp.int32, (128, n_exp), 1), 1.0, 0.0).astype(BF16)
     rwp_v[...] = jnp.dot(pick, rw_v[...], preferred_element_type=F32).astype(BF16)
     rb_p = lax.dot_general(jnp.broadcast_to(rb_v[...], (16, n_exp)), pick, transposed, preferred_element_type=F32)[0:1]
     expert = expert_of((1, 128), 1).astype(F32)
-    load_x.wait()
     norm = jnp.concatenate([norm_v[i:i + 1, :].astype(F32) for i in range(d_model // 128)], axis=1)
     tn = tok // 4
 
@@ -249,12 +263,16 @@
                         msg.start() if what == '!' else msg.wait_recv()
 
     def events(table, now):
-        for at, texts in table.items():
-            @pl.when(now == at)
-            def _(at=at, texts=texts):
-                with scope('event_' + str(at)):
-                    for text in texts:
-                        act(text)
+        for part in sorted({at // 4 for at in table}):
+            @pl.when(now // 4 == part)
+            def _(part=part):
+                for at, texts in table.items():
+                    if at // 4 == part:
+                        @pl.when(now == at)
+                        def _(at=at, texts=texts):
+                            with scope('event_' + str(at)):
+                                for text in texts:
+                                    act(text)
 
     with scope('bias_wait'):
         for msg in bias_msgs:
@@ -276,10 +294,7 @@
 
         @pl.when(last & (s < steps - 1))
         def _():
-            @pl.when(lax.rem(s, 2) == 1)
-            def _():
-                events(PHASE_1, s)
-
+            events(PHASE_1, s)
             q1, ch1 = step_of(s + 1)
 
             @pl.when((lax.rem(q1, 2) == 1) & ((s < 3) | (s >= 7)))
@@ -317,57 +332,86 @@
         cols = pl.ds(pl.multiple_of(j * COLS, COLS), COLS)
         return pltpu.make_async_copy(ostage.at[t], out_hbm.at[pl.ds(t * tm, tm), cols], out_sem.at[t])
 
-    def finish(j, wait_out):
+    def finish(j, t, wait_out):
         cols = pl.ds(pl.multiple_of(j * COLS, COLS), COLS)
+        pl.when(wait_out)(lambda: out_copy(j - 1, t).wait())
+        total = acc[lax.rem(j, 2), 2 + t] + rs_v[j, t]
+        ostage[t] = (x_v[pl.ds(t * tm, tm), cols].astype(F32) + total).astype(BF16)
+        out_copy(j, t).start()
+
+    def block_sum(j, rows):
+        total = None
+        for e in range(SLOTS):
+            w = wbuf[SLOTS // 2 * lax.rem(j, 2) + e // 2, d_ff * (e % 2):d_ff * (e % 2 + 1), :]
+            y = jnp.dot(z_v[e, rows, :], w, preferred_element_type=F32)
+            b = jnp.concatenate([bias_v[e, pl.ds(2 * groups + 2 * j, 1), :], bias_v[e, pl.ds(2 * groups + 2 * j + 1, 1), :]], axis=1)
+            y = (y + b).astype(BF16).astype(F32)
+            p = g_v[rows, e:e + 1]
+            term = jnp.where(p > 0, y * p, 0.0)
+            total = term if total is None else total + term
+        return total
+
+    final = blocks - 1
+
+    @pl.loop(0, 4 * final)
+    def _(i):
+        j, t = i // 4, lax.rem(i, 4)
+
+        @pl.when((t < 2) & (j >= 2))
+        def _():
+            sum_send(j - 2, t).wait_send()
+
+        events({at: texts for at, texts in PHASE_2.items() if at < 4 * final}, i)
+
+        @pl.when((t == 3) & (j >= 1))
+        def _():
+            with scope('finish'):
+                for half in range(2):
+                    sum_send(j - 1, half).wait_recv()
+                    finish(j - 1, half, j >= 2)
+
+        with scope('down'):
+            acc[lax.rem(j, 2), t] = block_sum(j, pl.ds(pl.multiple_of(t * tm, tm), tm))
+
+        @pl.when(t < 2)
+        def _():
+            sum_send(j, t).start()
+
+    with scope('event_final'):
+        for text in PHASE_2.get(4 * final, []):
+            act(text)
+    for t in range(2):
+        if final >= 2:
+            sum_send(final - 2, t).wait_send()
+
+    @pl.loop(0, 4)
+    def _(i):
+        with scope('down_far'):
+            acc[final % 2, i // 2, pl.ds(pl.multiple_of(tm // 2 * lax.rem(i, 2), tm // 2), tm // 2)] = block_sum(final, pl.ds(pl.multiple_of(tm // 2 * i, tm // 2), tm // 2))
+        last_sum_send(i).start()
+
+    @pl.loop(0, 2)
+    def _(t):
+        with scope('down_own'):
+            acc[final % 2, 2 + t] = block_sum(final, pl.ds(pl.multiple_of(tok + t * tm, tm), tm))
+
+    with scope('last_finish'):
         for t in range(2):
-            sum_send(j, t).wait_recv()
-            pl.when(wait_out)(lambda t=t: out_copy(j - 1, t).wait())
-            total = acc[lax.rem(j, 2), 2 + t] + rs_v[j, t]
-            ostage[t] = (x_v[pl.ds(t * tm, tm), cols].astype(F32) + total).astype(BF16)
-            out_copy(j, t).start()
-
-    @pl.loop(0, blocks)
-    def _(j):
-        par = lax.rem(j, 2)
-
-        @pl.loop(0, 4)
-        def _(t):
-            @pl.when((t < 2) & (j >= 2))
-            def _():
-                sum_send(j - 2, t).wait_send()
-
-            events({at: texts for at, texts in PHASE_2.items() if at < 4 * blocks}, 4 * j + t)
-
-            @pl.when((t == 3) & (j >= 1))
-            def _():
-                with scope('finish'):
-                    finish(j - 1, j >= 2)
-
-            rows = pl.ds(pl.multiple_of(t * tm, tm), tm)
-            with scope('down'):
-                total = None
-                for e in range(SLOTS):
-                    w = wbuf[SLOTS // 2 * par + e // 2, d_ff * (e % 2):d_ff * (e % 2 + 1), :]
-                    y = jnp.dot(z_v[e, rows, :], w, preferred_element_type=F32)
-                    b = jnp.concatenate([bias_v[e, pl.ds(2 * groups + 2 * j, 1), :], bias_v[e, pl.ds(2 * groups + 2 * j + 1, 1), :]], axis=1)
-                    y = (y + b).astype(BF16).astype(F32)
-                    p = g_v[rows, e:e + 1]
-                    term = jnp.where(p > 0, y * p, 0.0)
-                    total = term if total is None else total + term
-                acc[par, t] = total
-
-            @pl.when(t < 2)
-            def _():
-                sum_send(j, t).start()
-
-    with scope('last_finish'):
-        finish(blocks - 1, blocks >= 2)
+            if final:
+                sum_send(final - 1, t).wait_recv()
+                finish(final - 1, t, final >= 2)
         for t in range(2):
-            out_copy(blocks - 1, t).wait()
+            for i in range(2):
+                last_sum_send(2 * t + i).wait_recv()
+            finish(final, t, final >= 1)
+        for t in range(2):
+            out_copy(final, t).wait()
     with scope('drain'):
         for t in range(2):
-            for j in range(max(blocks - 2, 0), blocks):
-                sum_send(j, t).wait_send()
+            if final:
+                sum_send(final - 1, t).wait_send()
+        for i in range(4):
+            last_sum_send(i).wait_send()
         for q in range(SLOTS):
             for ch in range(2):
                 if q not in (0, 1, 2, 4, 6):
@@ -390,7 +434,6 @@
         assert w_gate_up.shape[0] == 1 and tok >= d_model
         groups, blocks, tm = 2 * d_ff // COLS, d_model // COLS, tok // 2
         hbm = pl.BlockSpec(memory_space=pltpu.HBM)
-        vmem = pl.BlockSpec(memory_space=pltpu.VMEM)
         wide = max(groups * 4, SLOTS * d_ff // d_model * 2)
         out = pl.pallas_call(
             kernel,
@@ -399,7 +442,7 @@
                 jax.ShapeDtypeStruct((SLOTS, groups, d_model, COLS), BF16),
                 jax.ShapeDtypeStruct((SLOTS, blocks, d_ff, COLS), BF16),
             ),
-            in_specs=[hbm, vmem, vmem, vmem, vmem, hbm, vmem, hbm, vmem],
+            in_specs=[hbm] * 9,
             out_specs=(hbm, hbm, hbm),
             scratch_shapes=[
                 pltpu.VMEM((SLOTS, 2 * tok, d_ff), BF16),
@@ -414,6 +457,12 @@
                 pltpu.VMEM((2, tm, COLS), BF16),
                 pltpu.VMEM((SLOTS, 2 * groups + d_model // 128, 128), F32),
                 pltpu.VMEM((128, d_model), BF16),
+                pltpu.VMEM(expert_ids.T.shape, jnp.int32),
+                pltpu.VMEM((d_model // 128, 128), BF16),
+                pltpu.VMEM(router_w.T.shape, BF16),
+                pltpu.VMEM(router_b[None].shape, BF16),
+                pltpu.VMEM(b_gate_up.shape, BF16),
+                pltpu.VMEM(b_down.shape, BF16),
             ],
             compiler_params=pltpu.CompilerParams(collective_id=0, has_side_effects=True, vmem_limit_bytes=67043328),
         )(x_in, expert_ids.T, norm_weight.reshape(-1, 128), router_w.T, router_b[None], w_gate_up, b_gate_up, w_down, b_down)

time: 219 us -> 212 us (0.968)
  Pallas kernels: 216 us -> 208 us
    pallas_call x1, Pallas kernels: 216 us -> 208 us  [local_block(): pl.pallas_call(kernel, out_shape=(jax.ShapeDtypeStruct((tok, d_model), BF...]
where the time goes in v4:
time: 212 us; the launch traced here: 211 us
  Pallas kernels  208 us (98%)
  local copies, waits for them, and re-layouts  3.08 us (1%)
    pallas_call x1, Pallas kernels, local_block(): pl.pallas_call(kernel, out_shape=(jax.ShapeDtypeStruct((tok, d_model), BF...  208 us

profile of v4, /device:TPU:97, one launch (start us, length us, event | category | flops | bytes accessed | tf_op | source)
XLA Modules:
  0.0 211.4 jit_solution(7912870940730658434)
XLA Ops:
  0.0 208.3 %shard_map.91 = (bf16[1024,1024]{1,0:T(8,128)(2,1)}, bf16[16,4,1024,256]{3,2,1,0:T(8,128)(2,1)}, bf16[16,4,512,256]{3,2,1,0:T(8,128)(2,1)}) custom-call(bf16[1024,1024]{1,0:T(8,128)(2,1)} %refs_0_.1, s32[8,1024]{1,0:T(8,128)} %bitcast.5, bf16[8,128]{1,0:T(8,128)(2,1)} %bitcast.6, bf16[32,1024]{1,0:T(8,128)(2,1)} %bitcast.4, bf16[1,32]{1,0:T(2,128)(2,1)} %bitcast.7, ...), custom_call_target="tpu_custom_call" | custom-call | tf_op jit(solution)/shard_map/pallas_call | solution.py:438
  208.3 3.1 %copy.11 = bf16[1024,1024]{1,0:T(8,128)(2,1)} copy(bf16[1024,1024]{1,0:T(8,128)(2,1)} %get-tuple-element.6) | data formatting | bytes 4194304

commit v5 on v4

--- a/solution.py
+++ b/solution.py
@@ -14,40 +14,42 @@
 RING = 4
 ORDER = [(0, 0), (0, 3), (0, 1), (1, 0), (0, 2), (1, 3), (1, 1), (1, 2)]
 SLOTS = 2 * len(ORDER)
-SCRATCH = 18
+SCRATCH = 20
 NAMES = 'aAbBcCdDeEfFgGhH'
 GATE_UP_WAYS = 'b0a+,b1a+,c0a-,c1a-,d0ay,d1ay,e0c-,e1b+,' + 'f0d+,f1by,g0d-,g1cy,h0g-,h1f+'
 DOWN_WAYS = 'b.a+,c.a-,d.ay,e0b+,e1c-,f.d+,g.d-,h0f+,h1g-'
-FIRST_WAYS = 'h0ey,h1ey'
+FIRST_WAYS, EARLY = 'h0ey,h1ey', 1
 STEPS = 'a0a1A0A1a0a1A0A1b1B1c0C0b0B0c1C1d0D0' + 'e0e1E0E1f1F1f0F0g0G0g1G1h1H1h0H0d1D1'
 PHASE_1 = {
-    3: ['~,!d0,?~'],
+    3: ['~,!d0,?~,*'],
     7: ['?b1,?c0,!e1,!e0,!f1,!B1,!C0'],
     11: ['?b0,?c1,!g1,!B0,!C1'],
-    13: ['?d0,!f0,!g0,!D0,!d.0,!d1'],
+    13: ['?d0,!f0,!g0,!D0,!d1'],
     17: ['!c.0,?e0,?e1,!E0,!E1,!d.1'],
-    21: ['?f1,!h1,!F1,!b.0'],
-    23: ['?f0,?g0,!h0,!F0,!G0'],
-    27: ['?g1,!G1,?d.0,!f.0,!g.0,!D.0'],
+    21: ['?f1,!h1,!F1,!b.0,!b.1'],
+    23: ['?f0,?g0,!h0,!F0,!G0,!c.1'],
+    27: ['?g1,!G1,?d.0,!D.0'],
     29: ['?h1,!H1'],
-    31: ['?h0,!H0', 'r0,!b.1,!c.1'],
-    33: ['?d1,!D1,?d.1,!f.1,!g.1,!D.1', '?f.0,?g.0,!F.0,!G.0'],
-    34: ['?e.0,!h.0,!E.0,!d.2,!d.3,!b.2,!c.2'],
+    31: ['?h0,!H0', 'r0,!f.0,!g.0'],
+    33: ['?d1,!D1,r1,?d.1,!f.1,!g.1,!D.1', '?e.0,!h.0,!E.0,!d.2,!b.2,!c.2'],
 }
 PHASE_2 = {
-    0: ['i0,j0,<e.0,r1,?h.0,!H.0,<h.0,s1,l0,w0'],
-    1: ['i1'],
-    2: ['?d.2,!f.2,!g.2,!D.2,r2,j1'],
-    3: ['k1'],
-    4: ['l1,w1'],
-    5: ['s2,!b.3,!c.3,?d.3,!f.3,!g.3,!D.3,i2'],
-    6: ['j2'],
-    7: ['k2'],
-    8: ['l2,w2'],
-    9: ['r3'],
-    10: ['s3,i3'],
-    11: ['j3'],
-    12: ['k3,l3,w3'],
+    0: ['?f.0,?g.0,!F.0,!G.0,i0,j0,<e.0', '?h.0,!H.0,<h.0,!d.3,l0,w0'],
+    1: ['s1,?d.2,!f.2,!g.2,!D.2,i1'],
+    2: ['?e.1,!E.1,j1'],
+    3: ['<e.1,?h.1,!H.1,<h.1,r2'],
+    4: ['l1'],
+    5: ['w1'],
+    6: ['s2,!b.3,!c.3,?d.3,!f.3,!g.3,!D.3,i2'],
+    7: ['j2'],
+    8: ['k2'],
+    9: ['l2'],
+    10: ['w2'],
+    11: ['r3'],
+    12: ['s3,i3'],
+    13: ['j3'],
+    14: ['k3'],
+    15: ['l3,w3'],
 }
 SHORT = {'r': '?b,?c,!e,!B,!C', 's': '?f,?g,!h,!F,!G', 'i': '<a,<b,<c,<d,<f,<g', 'j': '?A,<A,?B,<B,?C,<C,?D,<D,?F,<F,?G,<G',
          'k': '?e,!E,<e,?h,!H,<h', 'l': '?E,<E,?H,<H'}
@@ -56,11 +58,11 @@
 def kernel(*refs):
     wd = refs[len(refs) - SCRATCH - 1]
     slots, blocks = wd.shape[:2]
-    counts = [(slots, 2), (slots, 2), (slots, blocks, 2), (slots, blocks, 2), (slots,), (slots,), (2,), (2,), (blocks, 4), (blocks, 4), (8,), (2, slots), (8,), (2,)]
+    counts = [(slots, 2), (slots, 2), (slots, blocks, 2), (slots, blocks, 2), (slots,), (slots,), (2,), (2,), (blocks, 8), (blocks, 8), (8,), (2, slots), (8,), (2,), (8,)]
     pl.run_scoped(lambda *sems: body(*refs, *sems), *[pltpu.SemaphoreType.DMA(c) for c in counts])
 
 
-def body(x_hbm, ids_hbm, norm_hbm, rw_hbm, rb_hbm, wgu_hbm, bgu_hbm, wd_hbm, bd_hbm, out_hbm, wg, wd, z_v, h_v, wbuf, g_v, gfar, gsend, acc, rs_v, x_v, ostage, bias_v, rwp_v, ids_v, norm_v, rw_v, rb_v, bgu_v, bd_v, wg_s, wg_r, wd_s, wd_r, bias_s, bias_r, hg_s, hg_r, rs_s, rs_r, ld_sem, ld2_sem, in_sem, out_sem):
+def body(x_hbm, ids_hbm, norm_hbm, rw_hbm, rb_hbm, wgu_hbm, bgu_hbm, wd_hbm, bd_hbm, out_hbm, wg, wd, z_v, h_v, wbuf, g_v, gfar, gsend, acc, rs_v, x_v, ostage, late_v, bias_v, bias_b, rwp_v, ids_v, norm_v, rw_v, rb_v, bgu_v, bd_v, wg_s, wg_r, wd_s, wd_r, bias_s, bias_r, hg_s, hg_r, rs_s, rs_r, ld_sem, ld2_sem, in_sem, out_sem, last_sem):
     tok, d_model = x_hbm.shape
     d_ff = wd_hbm.shape[1]
     groups = 2 * d_ff // COLS
@@ -91,6 +93,7 @@
 
     gate_up_way, down_way, first_way = ways(GATE_UP_WAYS), ways(DOWN_WAYS), ways(FIRST_WAYS)
     relayed_slots = [NAMES.index(n) for n in 'eh']
+    late_slots = [NAMES.index(n) for n in 'eEhH']
 
     def target(way):
         if way == 's':
@@ -104,15 +107,20 @@
         here = wbuf.at[part] if static and src == 0 else wg.at[src, part]
         return remote(here, wg.at[q, part], wg_s.at[q, ch], wg_r.at[q, ch], target(way))
 
+    def place(q, j, rows=slice(None)):
+        if j == blocks - 1 and q in late_slots:
+            return late_v.at[late_slots.index(q), rows]
+        return wd.at[q, j, rows]
+
     def down(q, j):
         def one(half):
             src, way = down_way.get((q, half), (q - 1, 's'))
-            if j == 0:
+            if j < EARLY:
                 src, way = first_way.get((q, half), (src, way))
             rows = slice(None) if half == '.' else pl.ds(d_ff // 2 * int(half), d_ff // 2)
-            here = wd_hbm.at[0, :, pl.ds(j * COLS, COLS)] if src == 0 else wd.at[src, j, rows]
+            here = wd_hbm.at[0, :, pl.ds(j * COLS, COLS)] if src == 0 else place(src, j, rows)
             at = 0 if half == '.' else int(half)
-            return remote(here, wd.at[q, j, rows], wd_s.at[q, j, at], wd_r.at[q, j, at], target(way))
+            return remote(here, place(q, j, rows), wd_s.at[q, j, at], wd_r.at[q, j, at], target(way))
 
         return [one(half) for half in ('01' if q in relayed_slots else '.')]
 
@@ -123,13 +131,20 @@
         return remote(gsend, gfar, hg_s.at[1], hg_r.at[1], dev(away, 0))
 
     def bias_send(q, where):
-        return remote(bias_v.at[0], bias_v.at[q], bias_s.at[q], bias_r.at[q], where)
+        return remote(bias_b.at[0], bias_b.at[q], bias_s.at[q], bias_r.at[q], where)
 
     def sum_send(j, t):
         return remote(acc.at[lax.rem(j, 2), t], rs_v.at[j, t], rs_s.at[j, t], rs_r.at[j, t], dev(-away, 0))
 
+    pieces = 8
+    few = tok // pieces
+
+    def piece(i):
+        per_tile = pieces // 2
+        return i // per_tile, pl.ds(pl.multiple_of(few * lax.rem(i, per_tile), few), few)
+
     def last_sum_send(i):
-        j, t, rows = blocks - 1, i // 2, pl.ds(pl.multiple_of(tm // 2 * lax.rem(i, 2), tm // 2), tm // 2)
+        j, (t, rows) = blocks - 1, piece(i)
         return remote(acc.at[j % 2, t, rows], rs_v.at[j, t, rows], rs_s.at[j, i], rs_r.at[j, i], dev(-away, 0))
 
     raw = h_v.at[pl.ds(tok, tok)]
@@ -148,21 +163,26 @@
         bias_v[0, 2 * g + 1:2 * g + 2, :] = b[0:1, 128:]
     for i in range(d_model // 128):
         bias_v[0, 2 * groups + i:2 * groups + i + 1, :] = bd_v[:, 128 * i:128 * (i + 1)].astype(F32)
-    with scope('load_w'):
-        loads[0].wait()
+    bias_b[0] = bias_v[0].astype(BF16)
+    loads[0].wait()
     for g in range(groups):
         wbuf[g] = jnp.dot(raw[pl.ds(0, d_model), COLS * g:COLS * (g + 1)], split, preferred_element_type=F32).astype(BF16)
     with scope('barrier'):
         pl.semaphore_wait(pltpu.get_barrier_semaphore(), len(peers) + 2)
-    bias_msgs = []
+    def first_go(names):
+        for name in names.split(','):
+            gate_up(NAMES.index(name[0]), int(name[1])).start()
+
+    first_go('b1,c0')
+    bias_msgs = {}
     for s, dc in ORDER:
         for f in (0, 1):
             q = 2 * ORDER.index((s, (RING - dc) % RING)) + f
             if q:
-                bias_msgs.append(bias_send(q, dev(2 * s, dc, f)))
-                bias_msgs[-1].start()
-    for name in 'b1,c0,b0,c1,A0,A1'.split(','):
-        gate_up(NAMES.index(name[0]), int(name[1])).start()
+                bias_msgs[q] = bias_send(q, dev(2 * s, dc, f))
+                bias_msgs[q].start()
+    down(NAMES.index('d'), 0)[0].start()
+    first_go('b0,c1,A0,A1')
 
     def expert_of(shape, dim):
         lane = lax.broadcasted_iota(jnp.int32, shape, dim)
@@ -243,11 +263,14 @@
             what, name, rest = word[0], word[1:2], word[2:]
             if what == '~':
                 hidden_send().wait_send()
+            elif what == '*':
+                take_biases(range(2, SLOTS))
             elif name == '~':
                 hidden_send().wait_recv()
             elif what == 'w':
                 for q in range(SLOTS):
-                    down_load(int(name), q).wait()
+                    if int(name) < blocks - 1 or q not in late_slots:
+                        down_load(int(name), q).wait()
             elif what in SHORT:
                 if int(name) < blocks:
                     act(','.join(w + '.' + name for w in SHORT[what].split(',')))
@@ -257,7 +280,8 @@
             elif int(rest[1:]) < blocks:
                 q, j = NAMES.index(name), int(rest[1:])
                 if what == '<':
-                    down_load(j, q).start()
+                    if j < blocks - 1 or q not in late_slots:
+                        down_load(j, q).start()
                 else:
                     for msg in down(q, j):
                         msg.start() if what == '!' else msg.wait_recv()
@@ -274,50 +298,67 @@
                                 for text in texts:
                                     act(text)
 
+    def take_biases(qs):
+        for q in qs:
+            bias_msgs[q].wait_recv()
+            bias_v[q] = bias_b[q].astype(F32)
+
     with scope('bias_wait'):
-        for msg in bias_msgs:
-            msg.wait_recv()
-
-    @pl.loop(0, 8 + 2 * (steps - 8))
-    def _(i):
-        single = i < 8
-        s = jnp.where(single, i, 4 + i // 2)
+        take_biases([1])
+
+    def before_end(s):
+        events(PHASE_1, s)
+        q, ch = step_of(s + 1)
+
+        @pl.when((lax.rem(q, 2) == 1) & ((s < 3) | (s >= 7)))
+        def _():
+            with scope('sib_wait'):
+                gate_up(q, ch).wait_recv()
+
+        @pl.when(q > 0)
+        def _():
+            weights_load(s + 1).start()
+
+    def up(s, bases):
         q, ch = step_of(s)
-        first = single | (lax.rem(i, 2) == 0)
-        last = single | (lax.rem(i, 2) == 1)
-        foreign = jnp.where(single, i // 4, lax.rem(i, 2))
-
-        @pl.when(first & (q > 0))
-        def _():
-            with scope('load_wait'):
-                weights_load(s).wait()
-
-        @pl.when(last & (s < steps - 1))
-        def _():
-            events(PHASE_1, s)
-            q1, ch1 = step_of(s + 1)
-
-            @pl.when((lax.rem(q1, 2) == 1) & ((s < 3) | (s >= 7)))
-            def _():
-                with scope('sib_wait'):
-                    gate_up(q1, ch1).wait_recv()
-
-            @pl.when(q1 > 0)
-            def _():
-                weights_load(s + 1).start()
-
         w_at = half_g * buffer_of(s, q, ch)
         bias_at = half_g * 2 * ch
         with scope('up'):
-            for t in range(2):
-                rows = pl.ds(pl.multiple_of((1 - foreign) * tok + t * tm, tm), tm)
-                for g in range(half_g):
+            for g in range(half_g):
+                for base in bases:
+                    rows = pl.ds(pl.multiple_of(base, tm), tm)
                     u = jnp.dot(h_v[rows, :], wbuf[w_at + g], preferred_element_type=F32)
                     a = (u[:, :128] + bias_v[q, pl.ds(bias_at + 2 * g, 1), :]).astype(BF16)
                     l = (u[:, 128:] + bias_v[q, pl.ds(bias_at + 2 * g + 1, 1), :]).astype(BF16)
                     a = jnp.minimum(a, LIMIT).astype(F32)
                     l = jnp.clip(l, -LIMIT, LIMIT).astype(F32)
                     z_v[q, rows, pl.ds(pl.multiple_of(128 * (half_g * ch + g), 128), 128)] = (a * jax.nn.sigmoid(ALPHA * a) * (l + 1.0)).astype(BF16)
+
+    merged = steps - 6
+
+    @pl.loop(0, 2 * merged - 8)
+    def _(i):
+        single = i < 8
+        s = jnp.where(single, i, 4 + i // 2)
+        q, ch = step_of(s)
+        first = single | (lax.rem(i, 2) == 0)
+        foreign = jnp.where(single, i // 4, lax.rem(i, 2))
+
+        @pl.when(first & (q > 0))
+        def _():
+            weights_load(s).wait()
+
+        @pl.when(single | (lax.rem(i, 2) == 1))
+        def _():
+            before_end(s)
+
+        up(s, [(1 - foreign) * tok + t * tm for t in range(2)])
+
+    @pl.loop(merged, steps)
+    def _(s):
+        weights_load(s).wait()
+        pl.when(s < steps - 1)(lambda: before_end(s))
+        up(s, [t * tm for t in range(4)])
 
     with scope('own_sent'):
         for q in (2, 4, 6, 1):
@@ -339,10 +380,10 @@
         ostage[t] = (x_v[pl.ds(t * tm, tm), cols].astype(F32) + total).astype(BF16)
         out_copy(j, t).start()
 
-    def block_sum(j, rows):
+    def block_sum(j, rows, last=False):
         total = None
         for e in range(SLOTS):
-            w = wbuf[SLOTS // 2 * lax.rem(j, 2) + e // 2, d_ff * (e % 2):d_ff * (e % 2 + 1), :]
+            w = late_v[late_slots.index(e)] if last and e in late_slots else wbuf[SLOTS // 2 * lax.rem(j, 2) + e // 2, d_ff * (e % 2):d_ff * (e % 2 + 1), :]
             y = jnp.dot(z_v[e, rows, :], w, preferred_element_type=F32)
             b = jnp.concatenate([bias_v[e, pl.ds(2 * groups + 2 * j, 1), :], bias_v[e, pl.ds(2 * groups + 2 * j + 1, 1), :]], axis=1)
             y = (y + b).astype(BF16).astype(F32)
@@ -351,17 +392,18 @@
             total = term if total is None else total + term
         return total
 
-    final = blocks - 1
-
-    @pl.loop(0, 4 * final)
+    final, per_block = blocks - 1, 5
+
+    @pl.loop(0, per_block * final)
     def _(i):
-        j, t = i // 4, lax.rem(i, 4)
+        j, t = i // per_block, lax.rem(i, per_block)
+        par = lax.rem(j, 2)
 
         @pl.when((t < 2) & (j >= 2))
         def _():
             sum_send(j - 2, t).wait_send()
 
-        events({at: texts for at, texts in PHASE_2.items() if at < 4 * final}, i)
+        events({at: texts for at, texts in PHASE_2.items() if at < per_block * final}, i)
 
         @pl.when((t == 3) & (j >= 1))
         def _():
@@ -370,47 +412,68 @@
                     sum_send(j - 1, half).wait_recv()
                     finish(j - 1, half, j >= 2)
 
-        with scope('down'):
-            acc[lax.rem(j, 2), t] = block_sum(j, pl.ds(pl.multiple_of(t * tm, tm), tm))
+        @pl.when(t < 3)
+        def _():
+            with scope('down'):
+                acc[par, t] = block_sum(j, pl.ds(pl.multiple_of(t * tm, tm), tm))
 
         @pl.when(t < 2)
         def _():
             sum_send(j, t).start()
 
+        @pl.when(t >= 3)
+        def _():
+            at = pl.multiple_of(tm // 2 * (t - 3), tm // 2)
+            with scope('down_half'):
+                acc[par, 3, pl.ds(at, tm // 2)] = block_sum(j, pl.ds(pl.multiple_of(tok + tm + at, tm // 2), tm // 2))
+
     with scope('event_final'):
-        for text in PHASE_2.get(4 * final, []):
+        for text in PHASE_2.get(per_block * final, []):
             act(text)
     for t in range(2):
         if final >= 2:
             sum_send(final - 2, t).wait_send()
 
-    @pl.loop(0, 4)
+    @pl.loop(0, pieces)
     def _(i):
+        t, rows = piece(i)
         with scope('down_far'):
-            acc[final % 2, i // 2, pl.ds(pl.multiple_of(tm // 2 * lax.rem(i, 2), tm // 2), tm // 2)] = block_sum(final, pl.ds(pl.multiple_of(tm // 2 * i, tm // 2), tm // 2))
+            acc[final % 2, t, rows] = block_sum(final, pl.ds(pl.multiple_of(few * i, few), few), True)
         last_sum_send(i).start()
 
     @pl.loop(0, 2)
     def _(t):
         with scope('down_own'):
-            acc[final % 2, 2 + t] = block_sum(final, pl.ds(pl.multiple_of(tok + t * tm, tm), tm))
+            acc[final % 2, 2 + t] = block_sum(final, pl.ds(pl.multiple_of(tok + t * tm, tm), tm), True)
+
+    def last_copy(i):
+        t, rows = piece(i)
+        return pltpu.make_async_copy(ostage.at[t, rows], out_hbm.at[pl.ds(pl.multiple_of(few * i, few), few), pl.ds(COLS * final, COLS)], last_sem.at[i])
 
     with scope('last_finish'):
         for t in range(2):
             if final:
                 sum_send(final - 1, t).wait_recv()
                 finish(final - 1, t, final >= 2)
-        for t in range(2):
-            for i in range(2):
-                last_sum_send(2 * t + i).wait_recv()
-            finish(final, t, final >= 1)
-        for t in range(2):
-            out_copy(final, t).wait()
+        if final:
+            for t in range(2):
+                out_copy(final - 1, t).wait()
+
+        @pl.loop(0, pieces)
+        def _(i):
+            last_sum_send(i).wait_recv()
+            t, rows = piece(i)
+            total = acc[final % 2, 2 + t, rows] + rs_v[final, t, rows]
+            ostage[t, rows] = (x_v[pl.ds(pl.multiple_of(few * i, few), few), pl.ds(COLS * final, COLS)].astype(F32) + total).astype(BF16)
+            last_copy(i).start()
+
+        for i in range(pieces):
+            last_copy(i).wait()
     with scope('drain'):
         for t in range(2):
             if final:
                 sum_send(final - 1, t).wait_send()
-        for i in range(4):
+        for i in range(pieces):
             last_sum_send(i).wait_send()
         for q in range(SLOTS):
             for ch in range(2):
@@ -419,9 +482,22 @@
             for j in range(blocks if q else 0):
                 for msg in down(q, j):
                     msg.wait_send()
-        for msg in bias_msgs:
+        for msg in bias_msgs.values():
             msg.wait_send()
         gates_send().wait_send()
+
+
+def copy_out(src, dst, buf, in_sem, out_sem):
+    chunks, rows = buf.shape[:2]
+    loads = [pltpu.make_async_copy(src.at[pl.ds(rows * i, rows)], buf.at[i], in_sem.at[i]) for i in range(chunks)]
+    stores = [pltpu.make_async_copy(buf.at[i], dst.at[pl.ds(rows * i, rows)], out_sem.at[i]) for i in range(chunks)]
+    for load in loads:
+        load.start()
+    for load, store in zip(loads, stores):
+        load.wait()
+        store.start()
+    for store in stores:
+        store.wait()
 
 
 def solution(mesh):
@@ -455,7 +531,9 @@
                 pltpu.VMEM((blocks, 2, tm, COLS), F32),
                 pltpu.VMEM((tok, d_model), BF16),
                 pltpu.VMEM((2, tm, COLS), BF16),
+                pltpu.VMEM((4, d_ff, COLS), BF16),
                 pltpu.VMEM((SLOTS, 2 * groups + d_model // 128, 128), F32),
+                pltpu.VMEM((SLOTS, 2 * groups + d_model // 128, 128), BF16),
                 pltpu.VMEM((128, d_model), BF16),
                 pltpu.VMEM(expert_ids.T.shape, jnp.int32),
                 pltpu.VMEM((d_model // 128, 128), BF16),
@@ -466,6 +544,14 @@
             ],
             compiler_params=pltpu.CompilerParams(collective_id=0, has_side_effects=True, vmem_limit_bytes=67043328),
         )(x_in, expert_ids.T, norm_weight.reshape(-1, 128), router_w.T, router_b[None], w_gate_up, b_gate_up, w_down, b_down)
-        return out[0]
+        chunks = 8
+        return pl.pallas_call(
+            copy_out,
+            out_shape=jax.ShapeDtypeStruct((tok, d_model), BF16),
+            in_specs=[hbm],
+            out_specs=hbm,
+            scratch_shapes=[pltpu.VMEM((chunks, tok // chunks, d_model), BF16), pltpu.SemaphoreType.DMA((chunks,)), pltpu.SemaphoreType.DMA((chunks,))],
+            compiler_params=pltpu.CompilerParams(vmem_limit_bytes=60000000),
+        )(out[0])
 
     return jax.shard_map(local_block, mesh=mesh, in_specs=(rows_spec, rows_spec, P(), P(), P(), P('ep', None, None), P('ep', None), P('ep', None, None), P('ep', None)), out_specs=rows_spec, check_vma=False)

time: 212 us -> 208 us (0.981)
  local copies, waits for them, and re-layouts: 3.08 us -> 0 us
    pallas_call x1, Pallas kernels: 208 us -> 205 us  [local_block(): pl.pallas_call(kernel, out_shape=(jax.ShapeDtypeStruct((tok, d_model), BF...]
    unnamed x1 -> x0, local copies, waits for them, and re-layouts: 3.08 us -> none
    pallas_call x0 -> x1, Pallas kernels: none -> 2.39 us  [local_block(): pl.pallas_call(copy_out, out_shape=jax.ShapeDtypeStruct((tok, d_model), B...]
where the time goes in v5:
time: 208 us
  Pallas kernels  207 us (100%)
    pallas_call x1, Pallas kernels, local_block(): pl.pallas_call(kernel, out_shape=(jax.ShapeDtypeStruct((tok, d_model), BF...  205 us

profile of v5, /device:TPU:97, one launch (start us, length us, event | category | flops | bytes accessed | tf_op | source)
XLA Modules:
  0.0 207.7 jit_solution(2952204451230785625)
XLA Ops:
  0.0 205.1 %shard_map.91 = (bf16[1024,1024]{1,0:T(8,128)(2,1)}, bf16[16,4,1024,256]{3,2,1,0:T(8,128)(2,1)}, bf16[16,4,512,256]{3,2,1,0:T(8,128)(2,1)}) custom-call(bf16[1024,1024]{1,0:T(8,128)(2,1)} %refs_0_.1, s32[8,1024]{1,0:T(8,128)} %bitcast.5, bf16[8,128]{1,0:T(8,128)(2,1)} %bitcast.6, bf16[32,1024]{1,0:T(8,128)(2,1)} %bitcast.4, bf16[1,32]{1,0:T(2,128)(2,1)} %bitcast.7, ...), custom_call_target="tpu_custom_call" | custom-call | tf_op jit(solution)/shard_map/pallas_call | solution.py:514
  205.1 2.4 %shard_map.92 = bf16[1024,1024]{1,0:T(8,128)(2,1)} custom-call(bf16[1024,1024]{1,0:T(8,128)(2,1)} %get-tuple-element.6.src), custom_call_target="tpu_custom_call" | custom-call | tf_op jit(solution)/shard_map/pallas_call | solution.py:548

commit v6 on v5

--- a/solution.py
+++ b/solution.py
@@ -1,3 +1,6 @@
+import functools
+import math
+
 import jax
 import jax.numpy as jnp
 from jax import lax
@@ -11,14 +14,14 @@
 F32, BF16 = jnp.float32, jnp.bfloat16
 MESH = pl.DeviceIdType.MESH
 COLS = 256
-RING = 4
 ORDER = [(0, 0), (0, 3), (0, 1), (1, 0), (0, 2), (1, 3), (1, 1), (1, 2)]
 SLOTS = 2 * len(ORDER)
 SCRATCH = 20
 NAMES = 'aAbBcCdDeEfFgGhH'
 GATE_UP_WAYS = 'b0a+,b1a+,c0a-,c1a-,d0ay,d1ay,e0c-,e1b+,' + 'f0d+,f1by,g0d-,g1cy,h0g-,h1f+'
 DOWN_WAYS = 'b.a+,c.a-,d.ay,e0b+,e1c-,f.d+,g.d-,h0f+,h1g-'
-FIRST_WAYS, EARLY = 'h0ey,h1ey', 1
+FIRST_WAYS = 'h0ey,h1ey'
+SECOND_WAYS = 'h0f+,h1ey,h2ey,h3g-'
 STEPS = 'a0a1A0A1a0a1A0A1b1B1c0C0b0B0c1C1d0D0' + 'e0e1E0E1f1F1f0F0g0G0g1G1h1H1h0H0d1D1'
 PHASE_1 = {
     3: ['~,!d0,?~,*'],
@@ -34,9 +37,9 @@
     33: ['?d1,!D1,r1,?d.1,!f.1,!g.1,!D.1', '?e.0,!h.0,!E.0,!d.2,!b.2,!c.2'],
 }
 PHASE_2 = {
-    0: ['?f.0,?g.0,!F.0,!G.0,i0,j0,<e.0', '?h.0,!H.0,<h.0,!d.3,l0,w0'],
+    0: ['?f.0,?g.0,!F.0,!G.0,i0,j0,<e.0,?e.1,^h.1,!E.1', '?h.0,!H.0,<h.0,!d.3,l0,w0'],
     1: ['s1,?d.2,!f.2,!g.2,!D.2,i1'],
-    2: ['?e.1,!E.1,j1'],
+    2: ['j1'],
     3: ['<e.1,?h.1,!H.1,<h.1,r2'],
     4: ['l1'],
     5: ['w1'],
@@ -55,14 +58,14 @@
          'k': '?e,!E,<e,?h,!H,<h', 'l': '?E,<E,?H,<H'}
 
 
-def kernel(*refs):
+def kernel(ring, *refs):
     wd = refs[len(refs) - SCRATCH - 1]
     slots, blocks = wd.shape[:2]
-    counts = [(slots, 2), (slots, 2), (slots, blocks, 2), (slots, blocks, 2), (slots,), (slots,), (2,), (2,), (blocks, 8), (blocks, 8), (8,), (2, slots), (8,), (2,), (8,)]
-    pl.run_scoped(lambda *sems: body(*refs, *sems), *[pltpu.SemaphoreType.DMA(c) for c in counts])
-
-
-def body(x_hbm, ids_hbm, norm_hbm, rw_hbm, rb_hbm, wgu_hbm, bgu_hbm, wd_hbm, bd_hbm, out_hbm, wg, wd, z_v, h_v, wbuf, g_v, gfar, gsend, acc, rs_v, x_v, ostage, late_v, bias_v, bias_b, rwp_v, ids_v, norm_v, rw_v, rb_v, bgu_v, bd_v, wg_s, wg_r, wd_s, wd_r, bias_s, bias_r, hg_s, hg_r, rs_s, rs_r, ld_sem, ld2_sem, in_sem, out_sem, last_sem):
+    counts = [(slots, 2), (slots, 2), (slots, blocks, 4), (slots, blocks, 4), (slots,), (slots,), (2,), (2,), (blocks, 8), (blocks, 8), (8,), (2, slots), (8,), (2,), (8,)]
+    pl.run_scoped(lambda *sems: body(ring, *refs, *sems), *[pltpu.SemaphoreType.DMA(c) for c in counts])
+
+
+def body(ring, x_hbm, ids_hbm, norm_hbm, rw_hbm, rb_hbm, wgu_hbm, bgu_hbm, wd_hbm, bd_hbm, out_hbm, wg, wd, z_v, h_v, wbuf, g_v, gfar, gsend, acc, rs_v, x_v, ostage, late_v, bias_v, bias_b, rwp_v, ids_v, norm_v, rw_v, rb_v, bgu_v, bd_v, wg_s, wg_r, wd_s, wd_r, bias_s, bias_r, hg_s, hg_r, rs_s, rs_r, ld_sem, ld2_sem, in_sem, out_sem, last_sem):
     tok, d_model = x_hbm.shape
     d_ff = wd_hbm.shape[1]
     groups = 2 * d_ff // COLS
@@ -72,14 +75,14 @@
     top_k = ids_hbm.shape[0]
     me = lax.axis_index('ep')
     core = lax.rem(me, 2)
-    col = lax.rem(me // 2, RING)
-    row = me // (2 * RING)
+    col = lax.rem(me // 2, ring)
+    row = me // (2 * ring)
     away = 1 - 2 * core
     scope = jax.named_scope
 
     def dev(dy, dx, flip=0):
         other = 1 - core if flip else core
-        return {'ep': (lax.rem(row + dy + RING, RING) * RING + lax.rem(col + dx + RING, RING)) * 2 + other}
+        return {'ep': (lax.rem(row + dy + ring, ring) * ring + lax.rem(col + dx + ring, ring)) * 2 + other}
 
     peers = [(2 * s, dc, f) for s, dc in ORDER for f in (0, 1)][1:]
     for dy, dx, f in peers + [(1, 0, 0), (-1, 0, 0)]:
@@ -91,7 +94,8 @@
     def ways(table):
         return {(NAMES.index(m[0]), m[1]): (NAMES.index(m[2]), m[3]) for m in table.split(',')}
 
-    gate_up_way, down_way, first_way = ways(GATE_UP_WAYS), ways(DOWN_WAYS), ways(FIRST_WAYS)
+    gate_up_way, down_way = ways(GATE_UP_WAYS), ways(DOWN_WAYS)
+    early_ways = [ways(FIRST_WAYS), ways(SECOND_WAYS)]
     relayed_slots = [NAMES.index(n) for n in 'eh']
     late_slots = [NAMES.index(n) for n in 'eEhH']
 
@@ -112,17 +116,20 @@
             return late_v.at[late_slots.index(q), rows]
         return wd.at[q, j, rows]
 
+    def down_parts(q, j):
+        table = early_ways[j] if j < len(early_ways) and (q, '0') in early_ways[j] else down_way
+        parts = [p for p in '0123' if (q, p) in table] or ['.']
+        msgs = []
+        for at, part in enumerate(parts):
+            src, way = table.get((q, part), (q - 1, 's'))
+            few = d_ff // len(parts)
+            rows = slice(None) if part == '.' else pl.ds(few * at, few)
+            here = wd_hbm.at[0, :, pl.ds(j * COLS, COLS)] if src == 0 else place(src, j, rows)
+            msgs.append((remote(here, place(q, j, rows), wd_s.at[q, j, at], wd_r.at[q, j, at], target(way)), way))
+        return msgs
+
     def down(q, j):
-        def one(half):
-            src, way = down_way.get((q, half), (q - 1, 's'))
-            if j < EARLY:
-                src, way = first_way.get((q, half), (src, way))
-            rows = slice(None) if half == '.' else pl.ds(d_ff // 2 * int(half), d_ff // 2)
-            here = wd_hbm.at[0, :, pl.ds(j * COLS, COLS)] if src == 0 else place(src, j, rows)
-            at = 0 if half == '.' else int(half)
-            return remote(here, place(q, j, rows), wd_s.at[q, j, at], wd_r.at[q, j, at], target(way))
-
-        return [one(half) for half in ('01' if q in relayed_slots else '.')]
+        return [msg for msg, _ in down_parts(q, j)]
 
     def hidden_send():
         return remote(h_v.at[pl.ds(tok, tok)], h_v.at[pl.ds(0, tok)], hg_s.at[0], hg_r.at[0], dev(away, 0))
@@ -177,7 +184,7 @@
     bias_msgs = {}
     for s, dc in ORDER:
         for f in (0, 1):
-            q = 2 * ORDER.index((s, (RING - dc) % RING)) + f
+            q = 2 * ORDER.index((s, (ring - dc) % ring)) + f
             if q:
                 bias_msgs[q] = bias_send(q, dev(2 * s, dc, f))
                 bias_msgs[q].start()
@@ -187,13 +194,13 @@
     def expert_of(shape, dim):
         lane = lax.broadcasted_iota(jnp.int32, shape, dim)
         slot = lane & (SLOTS - 1)
-        class_row = jnp.where(lane < SLOTS, row, row + away + RING)
+        class_row = jnp.where(lane < SLOTS, row, row + away + ring)
         far = jnp.zeros_like(lane)
         side = jnp.zeros_like(lane)
         for m, (s, dc) in enumerate(ORDER):
             far = jnp.where(slot // 2 == m, 2 * s, far)
             side = jnp.where(slot // 2 == m, dc, side)
-        expert = (((class_row + far) & (RING - 1)) * RING + ((col + side) & (RING - 1))) * 2 + jnp.where((slot & 1) == 1, 1 - core, core)
+        expert = (((class_row + far) & (ring - 1)) * ring + ((col + side) & (ring - 1))) * 2 + jnp.where((slot & 1) == 1, 1 - core, core)
         return jnp.where(lane < 2 * SLOTS, expert, -1)
 
     for load in loads[3:]:
@@ -283,8 +290,12 @@
                     if j < blocks - 1 or q not in late_slots:
                         down_load(j, q).start()
                 else:
-                    for msg in down(q, j):
-                        msg.start() if what == '!' else msg.wait_recv()
+                    mixed = len({way for _, way in down_parts(q, j)} & set('+y')) == 2
+                    for msg, way in down_parts(q, j):
+                        if what == '?':
+                            msg.wait_recv()
+                        elif not mixed or (way == 'y') == (what == '^'):
+                            msg.start()
 
     def events(table, now):
         for part in sorted({at // 4 for at in table}):
@@ -502,7 +513,8 @@
 
 def solution(mesh):
     rows_spec = P(('dp', 'ep'), None)
-    assert mesh.shape['ep'] == 2 * RING * RING
+    ring = math.isqrt(mesh.shape['ep'] // 2)
+    assert 2 * ring * ring == mesh.shape['ep'] == 2 * SLOTS
 
     def local_block(x_in, expert_ids, norm_weight, router_w, router_b, w_gate_up, b_gate_up, w_down, b_down):
         tok, d_model = x_in.shape
@@ -512,7 +524,7 @@
         hbm = pl.BlockSpec(memory_space=pltpu.HBM)
         wide = max(groups * 4, SLOTS * d_ff // d_model * 2)
         out = pl.pallas_call(
-            kernel,
+            functools.partial(kernel, ring),
             out_shape=(
                 jax.ShapeDtypeStruct((tok, d_model), BF16),
                 jax.ShapeDtypeStruct((SLOTS, groups, d_model, COLS), BF16),

time: 208 us -> 207 us (level)
  no operation moved by 1% of the time
where the time goes in v6:
time: 207 us
  Pallas kernels  207 us (100%)
    pallas_call x1, Pallas kernels, local_block(): pl.pallas_call(functools.partial(kernel, ring), out_shape=(jax.ShapeDtype...  204 us

profile of v6, /device:TPU:97, one launch (start us, length us, event | category | flops | bytes accessed | tf_op | source)
XLA Modules:
  0.0 207.0 jit_solution(3298117865402547021)
XLA Ops:
  0.0 204.5 %shard_map.91 = (bf16[1024,1024]{1,0:T(8,128)(2,1)}, bf16[16,4,1024,256]{3,2,1,0:T(8,128)(2,1)}, bf16[16,4,512,256]{3,2,1,0:T(8,128)(2,1)}) custom-call(bf16[1024,1024]{1,0:T(8,128)(2,1)} %refs_0_.1, s32[8,1024]{1,0:T(8,128)} %bitcast.5, bf16[8,128]{1,0:T(8,128)(2,1)} %bitcast.6, bf16[32,1024]{1,0:T(8,128)(2,1)} %bitcast.4, bf16[1,32]{1,0:T(2,128)(2,1)} %bitcast.7, ...), custom_call_target="tpu_custom_call" | custom-call | tf_op jit(solution)/shard_map/pallas_call | solution.py:526
  204.5 2.4 %shard_map.92 = bf16[1024,1024]{1,0:T(8,128)(2,1)} custom-call(bf16[1024,1024]{1,0:T(8,128)(2,1)} %get-tuple-element.6.src), custom_call_target="tpu_custom_call" | custom-call | tf_op jit(solution)/shard_map/pallas_call | solution.py:560

commit v7 on v6

--- a/solution.py
+++ b/solution.py
@@ -28,7 +28,7 @@
     7: ['?b1,?c0,!e1,!e0,!f1,!B1,!C0'],
     11: ['?b0,?c1,!g1,!B0,!C1'],
     13: ['?d0,!f0,!g0,!D0,!d1'],
-    17: ['!c.0,?e0,?e1,!E0,!E1,!d.1'],
+    17: ['!c.0,?e0,?e1,!E0,!E1'],
     21: ['?f1,!h1,!F1,!b.0,!b.1'],
     23: ['?f0,?g0,!h0,!F0,!G0,!c.1'],
     27: ['?g1,!G1,?d.0,!D.0'],
@@ -40,19 +40,19 @@
     0: ['?f.0,?g.0,!F.0,!G.0,i0,j0,<e.0,?e.1,^h.1,!E.1', '?h.0,!H.0,<h.0,!d.3,l0,w0'],
     1: ['s1,?d.2,!f.2,!g.2,!D.2,i1'],
     2: ['j1'],
-    3: ['<e.1,?h.1,!H.1,<h.1,r2'],
-    4: ['l1'],
-    5: ['w1'],
-    6: ['s2,!b.3,!c.3,?d.3,!f.3,!g.3,!D.3,i2'],
-    7: ['j2'],
-    8: ['k2'],
-    9: ['l2'],
-    10: ['w2'],
-    11: ['r3'],
-    12: ['s3,i3'],
-    13: ['j3'],
-    14: ['k3'],
-    15: ['l3,w3'],
+    4: ['<e.1,?h.1,!H.1,<h.1,r2'],
+    5: ['l1'],
+    6: ['w1'],
+    7: ['s2,!b.3,!c.3,?d.3,!f.3,!g.3,!D.3,i2'],
+    8: ['j2'],
+    10: ['k2'],
+    11: ['l2'],
+    12: ['w2'],
+    13: ['r3'],
+    15: ['s3,i3'],
+    16: ['j3'],
+    17: ['%'],
+    18: ['&,w3'],
 }
 SHORT = {'r': '?b,?c,!e,!B,!C', 's': '?f,?g,!h,!F,!G', 'i': '<a,<b,<c,<d,<f,<g', 'j': '?A,<A,?B,<B,?C,<C,?D,<D,?F,<F,?G,<G',
          'k': '?e,!E,<e,?h,!H,<h', 'l': '?E,<E,?H,<H'}
@@ -116,20 +116,49 @@
             return late_v.at[late_slots.index(q), rows]
         return wd.at[q, j, rows]
 
-    def down_parts(q, j):
+    def down_ways(q, j):
         table = early_ways[j] if j < len(early_ways) and (q, '0') in early_ways[j] else down_way
-        parts = [p for p in '0123' if (q, p) in table] or ['.']
+        parts = [p for p in '0123' if (q, p) in table]
+        return [table[q, p] for p in parts] if parts else [table.get((q, '.'), (q - 1, 's'))]
+
+    def down(q, j, wanted='s+-y'):
+        parts = down_ways(q, j)
+        few = d_ff // len(parts)
         msgs = []
-        for at, part in enumerate(parts):
-            src, way = table.get((q, part), (q - 1, 's'))
-            few = d_ff // len(parts)
-            rows = slice(None) if part == '.' else pl.ds(few * at, few)
-            here = wd_hbm.at[0, :, pl.ds(j * COLS, COLS)] if src == 0 else place(src, j, rows)
-            msgs.append((remote(here, place(q, j, rows), wd_s.at[q, j, at], wd_r.at[q, j, at], target(way)), way))
+        for at, (src, way) in enumerate(parts):
+            if way in wanted:
+                rows = pl.ds(few * at, few)
+                here = wd_hbm.at[0, rows, pl.ds(j * COLS, COLS)] if src == 0 else place(src, j, rows)
+                there, slot, where = place(q, j, rows), q, target(way)
+                if j == blocks - 1 and q in relayed_slots:
+                    slot = q + 1 - core
+                    there = late_v.at[late_slots.index(q) + 1 - core, rows]
+                    where = {'ep': where['ep'] + 1 - core}
+                msgs.append(remote(here, there, wd_s.at[q, j, at], wd_r.at[slot, j, at], where))
         return msgs
 
-    def down(q, j):
-        return [msg for msg, _ in down_parts(q, j)]
+    def late_landed(q):
+        for half in range(2):
+            rows = pl.ds(d_ff // 2 * half, d_ff // 2)
+            spot = late_v.at[late_slots.index(q), rows]
+            remote(spot, spot, wd_s.at[q, blocks - 1, half], wd_r.at[q, blocks - 1, half], dev(0, 1)).wait_recv()
+
+    def late_handed(q):
+        at, other = late_slots.index(q), late_slots.index(q) ^ 1
+        return remote(late_v.at[at], late_v.at[other], wd_s.at[q, blocks - 1, 2], wd_r.at[q ^ 1, blocks - 1, 2], dev(0, 0, 1))
+
+    def hand_on(slots):
+        @pl.when(core == 1)
+        def _():
+            for q in slots:
+                late_landed(q)
+                late_handed(q).start()
+
+    def take_late():
+        @pl.when(core == 0)
+        def _():
+            for q in late_slots:
+                late_handed(q ^ 1).wait_recv()
 
     def hidden_send():
         return remote(h_v.at[pl.ds(tok, tok)], h_v.at[pl.ds(0, tok)], hg_s.at[0], hg_r.at[0], dev(away, 0))
@@ -162,6 +191,16 @@
     ri = lax.broadcasted_iota(jnp.int32, (COLS, COLS), 0)
     ci = lax.broadcasted_iota(jnp.int32, (COLS, COLS), 1)
     split = jnp.where(ri == jnp.where(ci < COLS // 2, 2 * ci, 2 * ci - (COLS - 1)), 1.0, 0.0).astype(BF16)
+    loads[0].wait()
+    for g in range(groups):
+        wbuf[g] = jnp.dot(raw[pl.ds(0, d_model), COLS * g:COLS * (g + 1)], split, preferred_element_type=F32).astype(BF16)
+    with scope('barrier'):
+        pl.semaphore_wait(pltpu.get_barrier_semaphore(), len(peers) + 2)
+    def first_go(names):
+        for name in names.split(','):
+            gate_up(NAMES.index(name[0]), int(name[1])).start()
+
+    first_go('b1,c0')
     for load in loads[1:3]:
         load.wait()
     for g in range(groups):
@@ -171,16 +210,6 @@
     for i in range(d_model // 128):
         bias_v[0, 2 * groups + i:2 * groups + i + 1, :] = bd_v[:, 128 * i:128 * (i + 1)].astype(F32)
     bias_b[0] = bias_v[0].astype(BF16)
-    loads[0].wait()
-    for g in range(groups):
-        wbuf[g] = jnp.dot(raw[pl.ds(0, d_model), COLS * g:COLS * (g + 1)], split, preferred_element_type=F32).astype(BF16)
-    with scope('barrier'):
-        pl.semaphore_wait(pltpu.get_barrier_semaphore(), len(peers) + 2)
-    def first_go(names):
-        for name in names.split(','):
-            gate_up(NAMES.index(name[0]), int(name[1])).start()
-
-    first_go('b1,c0')
     bias_msgs = {}
     for s, dc in ORDER:
         for f in (0, 1):
@@ -188,7 +217,8 @@
             if q:
                 bias_msgs[q] = bias_send(q, dev(2 * s, dc, f))
                 bias_msgs[q].start()
-    down(NAMES.index('d'), 0)[0].start()
+    for j in range(2):
+        down(NAMES.index('d'), j)[0].start()
     first_go('b0,c1,A0,A1')
 
     def expert_of(shape, dim):
@@ -274,6 +304,11 @@
                 take_biases(range(2, SLOTS))
             elif name == '~':
                 hidden_send().wait_recv()
+            elif what == '%':
+                hand_on(relayed_slots)
+            elif what == '&':
+                hand_on([q + 1 for q in relayed_slots])
+                take_late()
             elif what == 'w':
                 for q in range(SLOTS):
                     if int(name) < blocks - 1 or q not in late_slots:
@@ -290,12 +325,9 @@
                     if j < blocks - 1 or q not in late_slots:
                         down_load(j, q).start()
                 else:
-                    mixed = len({way for _, way in down_parts(q, j)} & set('+y')) == 2
-                    for msg, way in down_parts(q, j):
-                        if what == '?':
-                            msg.wait_recv()
-                        elif not mixed or (way == 'y') == (what == '^'):
-                            msg.start()
+                    mixed = len({way for _, way in down_ways(q, j)}) == 3
+                    for msg in down(q, j, {'?': 's+-y', '!': '+-' if mixed else 's+-y', '^': 'y'}[what]):
+                        msg.wait_recv() if what == '?' else msg.start()
 
     def events(table, now):
         for part in sorted({at // 4 for at in table}):
@@ -403,7 +435,7 @@
             total = term if total is None else total + term
         return total
 
-    final, per_block = blocks - 1, 5
+    final, per_block = blocks - 1, 6
 
     @pl.loop(0, per_block * final)
     def _(i):
@@ -416,14 +448,14 @@
 
         events({at: texts for at, texts in PHASE_2.items() if at < per_block * final}, i)
 
-        @pl.when((t == 3) & (j >= 1))
+        @pl.when((t == 4) & (j >= 1))
         def _():
             with scope('finish'):
                 for half in range(2):
                     sum_send(j - 1, half).wait_recv()
                     finish(j - 1, half, j >= 2)
 
-        @pl.when(t < 3)
+        @pl.when(t < 2)
         def _():
             with scope('down'):
                 acc[par, t] = block_sum(j, pl.ds(pl.multiple_of(t * tm, tm), tm))
@@ -432,11 +464,11 @@
         def _():
             sum_send(j, t).start()
 
-        @pl.when(t >= 3)
-        def _():
-            at = pl.multiple_of(tm // 2 * (t - 3), tm // 2)
+        @pl.when(t >= 2)
+        def _():
+            at = pl.multiple_of(tm // 2 * lax.rem(t, 2), tm // 2)
             with scope('down_half'):
-                acc[par, 3, pl.ds(at, tm // 2)] = block_sum(j, pl.ds(pl.multiple_of(tok + tm + at, tm // 2), tm // 2))
+                acc[par, 1 + t // 2, pl.ds(at, tm // 2)] = block_sum(j, pl.ds(pl.multiple_of(tok + tm * (t // 2 - 1) + at, tm // 2), tm // 2))
 
     with scope('event_final'):
         for text in PHASE_2.get(per_block * final, []):
@@ -491,8 +523,15 @@
                 if q not in (0, 1, 2, 4, 6):
                     gate_up(q, ch).wait_send()
             for j in range(blocks if q else 0):
-                for msg in down(q, j):
-                    msg.wait_send()
+                if j < blocks - 1 or q - 1 not in relayed_slots:
+                    for msg in down(q, j):
+                        msg.wait_send()
+
+        @pl.when(core == 1)
+        def _():
+            for q in late_slots:
+                late_handed(q).wait_send()
+
         for msg in bias_msgs.values():
             msg.wait_send()
         gates_send().wait_send()

time: 207 us -> 207 us (level)
  no operation moved by 1% of the time
where the time goes in v7:
time: 207 us
  Pallas kernels  207 us (100%)
    pallas_call x1, Pallas kernels, local_block(): pl.pallas_call(functools.partial(kernel, ring), out_shape=(jax.ShapeDtype...  205 us

profile of v7, /device:TPU:97, one launch (start us, length us, event | category | flops | bytes accessed | tf_op | source)
XLA Modules:
  0.0 207.2 jit_solution(12502514962720633233)
XLA Ops:
  0.0 204.6 %shard_map.91 = (bf16[1024,1024]{1,0:T(8,128)(2,1)}, bf16[16,4,1024,256]{3,2,1,0:T(8,128)(2,1)}, bf16[16,4,512,256]{3,2,1,0:T(8,128)(2,1)}) custom-call(bf16[1024,1024]{1,0:T(8,128)(2,1)} %refs_0_.1, s32[8,1024]{1,0:T(8,128)} %bitcast.5, bf16[8,128]{1,0:T(8,128)(2,1)} %bitcast.6, bf16[32,1024]{1,0:T(8,128)(2,1)} %bitcast.4, bf16[1,32]{1,0:T(2,128)(2,1)} %bitcast.7, ...), custom_call_target="tpu_custom_call" | custom-call | tf_op jit(solution)/shard_map/pallas_call | solution.py:565
  204.7 2.4 %shard_map.92 = bf16[1024,1024]{1,0:T(8,128)(2,1)} custom-call(bf16[1024,1024]{1,0:T(8,128)(2,1)} %get-tuple-element.6.src), custom_call_target="tpu_custom_call" | custom-call | tf_op jit(solution)/shard_map/pallas_call | solution.py:599
